TPU v7x, 128 devices: a whole 4x4x4 slice. The times are simulated.
128 devices in a mesh: node: 128 (over z, x, y, core).
Axes of the slice: x: 4, y: 4, z: 4, core: 2. Of those that a mesh axis runs over, the one named last changes fastest.
Arguments:
- labels: bfloat16 [524288, 512], P('node'), may hold values from -6 to 6
- seed_mask: int32 [524288], P('node'), may hold values 0 or 1
- band_w: bfloat16 [4096, 3, 128, 128], P('node'), may hold values from 0.0009994507 to 1
- far_block: int32 [128, 128, 2], P('node'), may hold values from 0 to 511
- far_tile: int32 [128, 128, 2], P('node'), may hold values from 0 to 31
- far_count: int32 [128, 128], P('node'), may hold values from 0 to 2, as said below
- far_w: bfloat16 [128, 128, 2, 8, 128], P('node'), may hold values from 0.049804688 to 2
Outputs:
- final_labels: bfloat16 [524288, 512], P('node')
- residual: float32 [2, 4096], P(None, 'node')
Inputs may be any that keep to these rules, and one draw needn't show every extreme that they name: `far_count`: in every draw at least one destination shard has all 2 slots live from every source shard; other counts vary from pair to pair.
All inputs are finite; a program needn't handle non-finite values. No bound on the sum of `seed_mask` on one device may be relied on, other than what follows from the above.
Results may differ from a plain program's by a relative error of at most 0.0027.
Values may be sent and summed in bfloat16 or wider, within the bound.
A program may use at most 128 MiB of HBM per device.

v0:
```python
import jax
import jax.numpy as jnp
from jax import lax
from jax.sharding import PartitionSpec as P

ITERS = 2


def with_halo(block, sides, width):
    for axis, dim in sides:
        count = lax.axis_size(axis)
        forward = [(i, i + 1) for i in range(count - 1)]
        forward.append((count - 1, 0))
        backward = [(target, source) for source, target in forward]
        low = lax.ppermute(
            lax.slice_in_dim(block, block.shape[dim] - width, None, axis=dim), axis, forward
        )
        high = lax.ppermute(lax.slice_in_dim(block, 0, width, axis=dim), axis, backward)
        block = jnp.concatenate([low, block, high], axis=dim)
    return block


def fetch_blocks(current, requests, block_rows, classes):
    blocks = current.reshape(-1, block_rows, classes)[requests]
    return lax.all_to_all(blocks, "node", split_axis=0, concat_axis=0, tiled=True)


def cycle_tiles(current, tile_count, tile_rows, classes):
    tiles = current.reshape(tile_count, tile_rows, classes)
    return with_halo(tiles, (("node", 0),), 1)


def body(labels, seed_mask, band_w, far_block, far_tile, far_count, far_w):
    node_rows, classes = labels.shape
    tile_count = band_w.shape[0]
    tile_rows = band_w.shape[2]
    peer_count = far_w.shape[1]
    slot_count = far_w.shape[2]
    block_rows = far_w.shape[3]
    requests = lax.all_to_all(far_block, "node", split_axis=1, concat_axis=0, tiled=True).reshape(
        peer_count, slot_count
    )
    live_slots = jnp.arange(slot_count)[None, :] < far_count[0][:, None]
    weights = jnp.where(live_slots[:, :, None, None], far_w[0], jnp.zeros((), jnp.bfloat16))
    flat_tiles = far_tile[0].reshape(-1)
    weight_sums = jnp.sum(weights, axis=2, dtype=jnp.float32).reshape(-1, tile_rows)
    degree_far = jnp.zeros((tile_count, tile_rows), jnp.float32).at[flat_tiles].add(weight_sums)
    degree = jnp.sum(band_w, axis=(1, 3), dtype=jnp.float32) + degree_far
    slot_weights = weights.reshape(peer_count * slot_count, block_rows, tile_rows)
    onehot = jnp.arange(tile_count)[:, None] == flat_tiles[None, :]
    placed = jnp.where(onehot[:, :, None, None], slot_weights[None], jnp.zeros((), jnp.bfloat16))
    placed = placed.reshape(tile_count, peer_count * slot_count * block_rows, tile_rows)
    seeded = (seed_mask == 1).reshape(tile_count, tile_rows, 1)
    clamped = labels.astype(jnp.float32).reshape(tile_count, tile_rows, classes)
    current = labels
    residuals = []
    for sweep in range(ITERS):
        padded = cycle_tiles(current, tile_count, tile_rows, classes)
        received = fetch_blocks(current, requests, block_rows, classes)
        band_sum = jnp.zeros((tile_count, tile_rows, classes), jnp.float32)
        for offset in (-1, 0, 1):
            source = padded[1 + offset : 1 + offset + tile_count]
            band_sum = band_sum + jnp.einsum(
                "itr,irc->itc", band_w[:, offset + 1], source, preferred_element_type=jnp.float32
            )
        far_sum = jnp.einsum(
            "tqr,qc->trc", placed, received.reshape(-1, classes), preferred_element_type=jnp.float32
        )
        averaged = (band_sum + far_sum) / degree[:, :, None]
        row_scale = jnp.sqrt(jnp.mean(averaged * averaged, axis=2, keepdims=True))
        scaled = averaged / jnp.maximum(row_scale, 0.05)
        fresh = jnp.where(seeded, clamped, scaled).astype(jnp.bfloat16)
        previous = current.astype(jnp.float32).reshape(tile_count, tile_rows, classes)
        residuals.append(jnp.sum(jnp.abs(fresh.astype(jnp.float32) - previous), axis=(1, 2)))
        current = fresh.reshape(node_rows, classes)
    return (current, jnp.stack(residuals))


def solution(mesh):
    placed = (
        P("node", None),
        P("node"),
        P("node", None, None, None),
        P("node", None, None),
        P("node", None, None),
        P("node", None),
        P("node", None, None, None, None),
    )
    return jax.shard_map(
        body,
        mesh=mesh,
        in_specs=placed,
        out_specs=(P("node", None), P(None, "node")),
        check_vma=False,
    )
```

profile of v0, /device:TPU:0, one launch (start us, length us, event | category | flops | bytes accessed | tf_op | source)
XLA Modules:
  0.0 184.5 jit_solution(16199250453833278590)
XLA Ops:
  0.6 1.4 copy.27
  2.0 11.2 %all-to-all-start = ((s32[1,128,2]{2,0,1:T(1,128)}), s32[1,128,2]{2,0,1:T(1,128)S(1)}, u32[]{:S(2)}, u32[]{:S(2)}) async-start(s32[1,128,2]{2,0,1:T(1,128)} %copy.27), calls=%async_computation | async-start | bytes 131072 | tf_op jit(solution)/shard_map/all_to_all | solution.py:40
  13.2 1.0 slice_bitcast_fusion
  14.2 7.1 %collective-permute-start.1 = (bf16[1,128,512]{2,1,0:T(8,128)(2,1)S(1)}, bf16[1,128,512]{2,1,0:T(8,128)(2,1)S(1)}, u32[]{:S(2)}, u32[]{:S(2)}) collective-permute-start(bf16[1,128,512]{2,1,0:T(8,128)(2,1)S(1)} %get-tuple-element.6), channel_id=1, source_target_pairs={{1,0},{2,1},{3,2},{4,3},{5,4},{6,5},{7,6},{8,7},{9,8},{10,9},{11,1... | collective-permute-start | bytes 393224 | tf_op jit(solution)/shard_map/ppermute | solution.py:18
  21.3 0.7 iota_compare_fusion.1
  22.4 0.8 copy.24
  23.4 1.4 bitcast_select_fusion.1
  25.1 4.3 %gather_fusion = bf16[256,8,512]{2,1,0:T(8,128)(2,1)} fusion(bf16[512,8,512]{2,1,0:T(8,128)(2,1)} %bitcast.75, s32[1024]{0:T(1024)S(1)} %pad_clamp_fusion), kind=kCustom, calls=%fused_computation | custom fusion | bytes 4195328 | tf_op jit(solution)/shard_map/gather | solution.py:24
  29.4 9.6 %all-to-all-start.1 = ((bf16[128,2,8,512]{3,2,1,0:T(8,128)(2,1)}), bf16[128,2,8,512]{3,2,1,0:T(8,128)(2,1)}, u32[]{:S(2)}, u32[]{:S(2)}) async-start(bf16[128,2,8,512]{3,2,1,0:T(8,128)(2,1)} %bitcast.14), calls=%async_computation.1 | async-start | bytes 4194304 | tf_op jit(solution)/shard_map/all_to_all | solution.py:25
  39.3 0.3 copy.25
  39.6 0.2 copy.26
  39.9 0.5 convert_reduce_fusion.1
  40.4 2.5 %convert_reduce_fusion = f32[32,128]{1,0:T(8,128)S(1)} fusion(bf16[32,3,128,128]{3,2,1,0:T(8,128)(2,1)} %param.9), kind=kLoop, calls=%fused_computation.29 | loop fusion | flops 3141632 | bytes 3162112 | tf_op jit(solution)/shard_map/reduce_sum | solution.py:48
  42.9 2.1 %scatter_fusion = f32[32,128]{1,0:T(8,128)S(1)} fusion(f32[32,128]{1,0:T(8,128)S(1)} %convert_reduce_fusion, s32[256]{0:T(256)S(1)} %bitcast.85, f32[256,128]{1,0:T(8,128)S(1)} %bitcast.83), kind=kCustom, calls=%fused_computation.2 | custom fusion | flops 32768 | bytes 394240 | tf_op jit(solution)/shard_map/scatter-add | solution.py:47
  45.1 7.1 %fusion.29 = f32[32,128,512]{2,1,0:T(8,128)} fusion(bf16[32,128,512]{2,1,0:T(8,128)(2,1)} %bitcast.76, bf16[32,3,128,128]{3,2,1,0:T(8,128)(2,1)} %param.9), kind=kOutput, calls=%fused_computation.46 | convolution fusion | flops 536870912 | bytes 13631488 | tf_op jit(solution)/shard_map/itr,irc->itc/dot_general | solution.py:63
  52.2 5.7 %fusion.23 = f32[32,512,128]{1,2,0:T(8,128)} fusion(bf16[32,128,512]{2,1,0:T(8,128)(2,1)S(1)} %bitcast.77, bf16[1,128,512]{2,1,0:T(8,128)(2,1)S(1)} %collective-permute-done, bf16[32,3,128,128]{3,2,1,0:T(8,128)(2,1)} %param.9), kind=kOutput, calls=%fused_computation.40 | convolution fusion | flops 545259520 | bytes 13762560 | tf_op jit(solution)/shard_map/itr,irc->itc/dot_general | solution.py:63
  57.9 11.0 %all-to-all-done.1 = bf16[128,2,8,512]{3,2,1,0:T(8,128)(2,1)} async-done(((bf16[128,2,8,512]{3,2,1,0:T(8,128)(2,1)}), bf16[128,2,8,512]{3,2,1,0:T(8,128)(2,1)}, u32[]{:S(2)}, u32[]{:S(2)}) %all-to-all-start.1) | async-done | bytes 2097184 | tf_op jit(solution)/shard_map/all_to_all | solution.py:25
  68.9 12.9 %fusion.2 = f32[32,128,512]{2,1,0:T(8,128)} fusion(bf16[2048,512,1]{1,0,2:T(8,128)(2,1)} %bitcast.16, pred[32,2048]{1,0:T(8,128)(4,1)S(1)} %copy.25, bf16[2048,128]{0,1:T(8,128)(2,1)S(1)} %copy.26), kind=kOutput, calls=%fused_computation.5 | convolution fusion | flops 8598323200 | bytes 11075584 | tf_op jit(solution)/shard_map/tqr,qc->trc/dot_general | solution.py:66
  81.8 13.5 %multiply_reduce_fusion.1 = (f32[32,128]{1,0:T(8,128)S(1)}, f32[32,128,512]{2,1,0:T(8,128)}) fusion(f32[32,128]{1,0:T(8,128)S(1)} %scatter_fusion, f32[32,128,512]{2,1,0:T(8,128)} %fusion.2, bf16[1,128,512]{2,1,0:T(8,128)(2,1)S(1)} %collective-permute-done.1, bf16[32,128,512]{2,1,0:T(8,128)(2,1)S(1)} %bitcast.78, bf16[32,3,128,128]{3,2,1,0:T(8,128)(2,1)} %param.9, ...), kind=kOutput, calls=%fused_computation.24 | convolution fusion | flops 557838336 | bytes 38961152 | tf_op jit(solution)/shard_map/itr,irc->itc/dot_general | solution.py:63
  95.4 7.1 %fusion.8 = bf16[32,128,512]{2,1,0:T(8,128)(2,1)} fusion(f32[32,128,512]{2,1,0:T(8,128)} %get-tuple-element.9, f32[32,128]{1,0:T(8,128)S(1)} %maximum_multiply_fusion.1, pred[32,128]{1,0:T(8,128)(4,1)S(1)} %compare_bitcast_fusion, bf16[4096,512]{1,0:T(8,128)(2,1)S(1)} %copy-done.1), kind=kLoop, calls=%fused_computation.15 | loop fusion | flops 8388608 | bytes 16797696 | tf_op jit(solution)/shard_map/convert_element_type | solution.py:72
  102.5 4.3 %gather_fusion.1 = bf16[256,8,512]{2,1,0:T(8,128)(2,1)} fusion(bf16[512,8,512]{2,1,0:T(8,128)(2,1)} %bitcast.80, s32[1024]{0:T(1024)S(1)} %pad_clamp_fusion), kind=kCustom, calls=%fused_computation.1 | custom fusion | bytes 4195328 | tf_op jit(solution)/shard_map/gather | solution.py:24
  106.8 5.8 %all-to-all-start.2 = ((bf16[128,2,8,512]{3,2,1,0:T(8,128)(2,1)}), bf16[128,2,8,512]{3,2,1,0:T(8,128)(2,1)}, u32[]{:S(2)}, u32[]{:S(2)}) async-start(bf16[128,2,8,512]{3,2,1,0:T(8,128)(2,1)} %bitcast.82), calls=%async_computation.2 | async-start | bytes 4194304 | tf_op jit(solution)/shard_map/all_to_all | solution.py:25
  112.6 1.0 fusion.45
  113.7 7.1 %fusion.27 = f32[32,512,128]{1,2,0:T(8,128)} fusion(bf16[32,128,512]{2,1,0:T(8,128)(2,1)} %fusion.8, bf16[32,3,128,128]{3,2,1,0:T(8,128)(2,1)} %param.9), kind=kOutput, calls=%fused_computation.44 | convolution fusion | flops 536870912 | bytes 13631488 | tf_op jit(solution)/shard_map/itr,irc->itc/dot_general | solution.py:63
  120.8 7.2 %collective-permute-start.3 = (bf16[1,128,512]{2,1,0:T(8,128)(2,1)S(1)}, bf16[1,128,512]{2,1,0:T(8,128)(2,1)S(1)}, u32[]{:S(2)}, u32[]{:S(2)}) collective-permute-start(bf16[1,128,512]{2,1,0:T(8,128)(2,1)S(1)} %get-tuple-element.4), channel_id=1, source_target_pairs={{1,0},{2,1},{3,2},{4,3},{5,4},{6,5},{7,6},{8,7},{9,8},{10,9},{11,1... | collective-permute-start | bytes 393224 | tf_op jit(solution)/shard_map/ppermute | solution.py:18
  127.9 15.6 %collective-permute-done.2 = bf16[1,128,512]{2,1,0:T(8,128)(2,1)S(1)} collective-permute-done((bf16[1,128,512]{2,1,0:T(8,128)(2,1)S(1)}, bf16[1,128,512]{2,1,0:T(8,128)(2,1)S(1)}, u32[]{:S(2)}, u32[]{:S(2)}) %collective-permute-start.2) | collective-permute-done | bytes 131104 | tf_op jit(solution)/shard_map/ppermute | solution.py:15
  143.6 5.7 %fusion.19 = f32[32,512,128]{1,2,0:T(8,128)} fusion(bf16[32,128,512]{2,1,0:T(8,128)(2,1)S(1)} %copy-done.3, bf16[1,128,512]{2,1,0:T(8,128)(2,1)S(1)} %collective-permute-done.2, bf16[32,3,128,128]{3,2,1,0:T(8,128)(2,1)} %param.9), kind=kOutput, calls=%fused_computation.34 | convolution fusion | flops 545259520 | bytes 13762560 | tf_op jit(solution)/shard_map/itr,irc->itc/dot_general | solution.py:63
  149.3 12.9 %fusion = f32[32,128,512]{2,1,0:T(8,128)} fusion(bf16[2048,512,1]{1,0,2:T(8,128)(2,1)} %bitcast.24, pred[32,2048]{1,0:T(8,128)(4,1)S(1)} %copy.25, bf16[2048,128]{0,1:T(8,128)(2,1)S(1)} %copy.26), kind=kOutput, calls=%fused_computation.3 | convolution fusion | flops 8598323200 | bytes 11075584 | tf_op jit(solution)/shard_map/tqr,qc->trc/dot_general | solution.py:66
  162.2 13.7 %multiply_reduce_fusion = (f32[32,128]{1,0:T(8,128)S(1)}, f32[32,128,512]{2,1,0:T(8,128)}) fusion(f32[32,128]{1,0:T(8,128)S(1)} %scatter_fusion, f32[32,128,512]{2,1,0:T(8,128)} %fusion, bf16[1,128,512]{2,1,0:T(8,128)(2,1)S(1)} %collective-permute-done.3, bf16[32,128,512]{2,1,0:T(8,128)(2,1)S(1)} %copy-done.4, bf16[32,3,128,128]{3,2,1,0:T(8,128)(2,1)} %param.9, ...), kind=kOutput, calls=%fused_computation.23 | convolution fusion | flops 557838336 | bytes 38961152 | tf_op jit(solution)/shard_map/itr,irc->itc/dot_general | solution.py:63
  175.9 5.0 %fusion.9 = bf16[32,128,512]{2,1,0:T(8,128)(2,1)S(1)} fusion(f32[32,128,512]{2,1,0:T(8,128)} %get-tuple-element.11, f32[32,128]{1,0:T(8,128)S(1)} %maximum_multiply_fusion, pred[32,128]{1,0:T(8,128)(4,1)S(1)} %compare_bitcast_fusion, bf16[4096,512]{1,0:T(8,128)(2,1)S(1)} %copy-done.2), kind=kLoop, calls=%fused_computation.16 | loop fusion | flops 8388608 | bytes 16797696 | tf_op jit(solution)/shard_map/convert_element_type | solution.py:72
  180.9 3.1 %fusion.11 = (f32[32]{0:T(128)S(1)}, f32[32]{0:T(128)S(1)}) fusion(bf16[32,128,512]{2,1,0:T(8,128)(2,1)S(1)} %bitcast.79, bf16[32,128,512]{2,1,0:T(8,128)(2,1)S(1)} %copy-done.4, bf16[32,128,512]{2,1,0:T(8,128)(2,1)S(1)} %fusion.9), kind=kLoop, calls=%fused_computation.18 | loop fusion | flops 18874304 | bytes 12583168 | tf_op jit(solution)/shard_map/reduce_sum | solution.py:74
  183.9 0.6 pad_maximum_fusion.12
  (37 shorter events, 1.2 us)
Async XLA Ops:
  2.0 22.8 %all-to-all-start = ((s32[1,128,2]{2,0,1:T(1,128)}), s32[1,128,2]{2,0,1:T(1,128)S(1)}, u32[]{:S(2)}, u32[]{:S(2)}) async-start(s32[1,128,2]{2,0,1:T(1,128)} %copy.27), calls=%async_computation | async-start | bytes 131072 | tf_op jit(solution)/shard_map/all_to_all | solution.py:40
  14.2 67.6 %collective-permute-start.1 = (bf16[1,128,512]{2,1,0:T(8,128)(2,1)S(1)}, bf16[1,128,512]{2,1,0:T(8,128)(2,1)S(1)}, u32[]{:S(2)}, u32[]{:S(2)}) collective-permute-start(bf16[1,128,512]{2,1,0:T(8,128)(2,1)S(1)} %get-tuple-element.6), channel_id=1, source_target_pairs={{1,0},{2,1},{3,2},{4,3},{5,4},{6,5},{7,6},{8,7},{9,8},{10,9},{11,1... | collective-permute-start | bytes 393224 | tf_op jit(solution)/shard_map/ppermute | solution.py:18
  21.3 30.9 %collective-permute-start = (bf16[1,128,512]{2,1,0:T(8,128)(2,1)S(1)}, bf16[1,128,512]{2,1,0:T(8,128)(2,1)S(1)}, u32[]{:S(2)}, u32[]{:S(2)}) collective-permute-start(bf16[1,128,512]{2,1,0:T(8,128)(2,1)S(1)} %get-tuple-element.7), channel_id=1, source_target_pairs={{0,1},{1,2},{2,3},{3,4},{4,5},{5,6},{6,7},{7,8},{8,9},{9,10},{10,1... | collective-permute-start | bytes 393224 | tf_op jit(solution)/shard_map/ppermute | solution.py:15
  25.0 14.8 %copy-start.6 = (bf16[1,128,2,8,128]{4,3,2,1,0:T(8,128)(2,1)S(1)}, bf16[1,128,2,8,128]{4,3,2,1,0:T(8,128)(2,1)}, u32[]{:S(2)}) copy-start(bf16[1,128,2,8,128]{4,3,2,1,0:T(8,128)(2,1)} %param.13) | copy-start | bytes 1572868
  29.4 39.5 %all-to-all-start.1 = ((bf16[128,2,8,512]{3,2,1,0:T(8,128)(2,1)}), bf16[128,2,8,512]{3,2,1,0:T(8,128)(2,1)}, u32[]{:S(2)}, u32[]{:S(2)}) async-start(bf16[128,2,8,512]{3,2,1,0:T(8,128)(2,1)} %bitcast.14), calls=%async_computation.1 | async-start | bytes 4194304 | tf_op jit(solution)/shard_map/all_to_all | solution.py:25
  45.0 7.2 %copy-start.7 = (s32[4096]{0:T(1024)S(1)}, s32[4096]{0:T(1024)}, u32[]{:S(2)}) copy-start(s32[4096]{0:T(1024)} %param.8) | copy-start | bytes 49156
  45.0 7.2 %copy-start = (bf16[4096,512]{1,0:T(8,128)(2,1)S(1)}, bf16[4096,512]{1,0:T(8,128)(2,1)}, u32[]{:S(2)}) copy-start(bf16[4096,512]{1,0:T(8,128)(2,1)} %param.7) | copy-start | bytes 12582916
  68.9 12.9 %copy-start.1 = (bf16[4096,512]{1,0:T(8,128)(2,1)S(1)}, bf16[4096,512]{1,0:T(8,128)(2,1)}, u32[]{:S(2)}) copy-start(bf16[4096,512]{1,0:T(8,128)(2,1)} %param.7) | copy-start | bytes 12582916
  106.8 42.5 %all-to-all-start.2 = ((bf16[128,2,8,512]{3,2,1,0:T(8,128)(2,1)}), bf16[128,2,8,512]{3,2,1,0:T(8,128)(2,1)}, u32[]{:S(2)}, u32[]{:S(2)}) async-start(bf16[128,2,8,512]{3,2,1,0:T(8,128)(2,1)} %bitcast.82), calls=%async_computation.2 | async-start | bytes 4194304 | tf_op jit(solution)/shard_map/all_to_all | solution.py:25
  113.6 30.0 %copy-start.3 = (bf16[32,128,512]{2,1,0:T(8,128)(2,1)S(1)}, bf16[32,128,512]{2,1,0:T(8,128)(2,1)}, u32[]{:S(2)}) copy-start(bf16[32,128,512]{2,1,0:T(8,128)(2,1)} %fusion.8) | copy-start | bytes 12582916
  113.6 30.0 %collective-permute-start.2 = (bf16[1,128,512]{2,1,0:T(8,128)(2,1)S(1)}, bf16[1,128,512]{2,1,0:T(8,128)(2,1)S(1)}, u32[]{:S(2)}, u32[]{:S(2)}) collective-permute-start(bf16[1,128,512]{2,1,0:T(8,128)(2,1)S(1)} %get-tuple-element.5), channel_id=1, source_target_pairs={{0,1},{1,2},{2,3},{3,4},{4,5},{5,6},{6,7},{7,8},{8,9},{9,10},{10,1... | collective-permute-start | bytes 393224 | tf_op jit(solution)/shard_map/ppermute | solution.py:15
  120.8 41.4 %collective-permute-start.3 = (bf16[1,128,512]{2,1,0:T(8,128)(2,1)S(1)}, bf16[1,128,512]{2,1,0:T(8,128)(2,1)S(1)}, u32[]{:S(2)}, u32[]{:S(2)}) collective-permute-start(bf16[1,128,512]{2,1,0:T(8,128)(2,1)S(1)} %get-tuple-element.4), channel_id=1, source_target_pairs={{1,0},{2,1},{3,2},{4,3},{5,4},{6,5},{7,6},{8,7},{9,8},{10,9},{11,1... | collective-permute-start | bytes 393224 | tf_op jit(solution)/shard_map/ppermute | solution.py:18
  149.3 12.9 %copy-start.4 = (bf16[32,128,512]{2,1,0:T(8,128)(2,1)S(1)}, bf16[32,128,512]{2,1,0:T(8,128)(2,1)}, u32[]{:S(2)}) copy-start(bf16[32,128,512]{2,1,0:T(8,128)(2,1)} %fusion.8) | copy-start | bytes 12582916
  162.2 13.7 %copy-start.2 = (bf16[4096,512]{1,0:T(8,128)(2,1)S(1)}, bf16[4096,512]{1,0:T(8,128)(2,1)}, u32[]{:S(2)}) copy-start(bf16[4096,512]{1,0:T(8,128)(2,1)} %param.7) | copy-start | bytes 12582916
  180.9 3.1 %copy-start.5 = (bf16[32,128,512]{2,1,0:T(8,128)(2,1)}, bf16[32,128,512]{2,1,0:T(8,128)(2,1)S(1)}, u32[]{:S(2)}) copy-start(bf16[32,128,512]{2,1,0:T(8,128)(2,1)S(1)} %fusion.9) | copy-start | bytes 12582916
where the time goes:
time: 185 us
  matrix products  78.7 us (43%)
  starting transfers between devices  40.9 us (22%)
  waiting for transfers between devices  26.7 us (14%)
  other arithmetic  23.1 us (12%)
  local copies, waits for them, and re-layouts  14.3 us (8%)
    dot_general x6, matrix products, body(): jnp.einsum('itr,irc->itc', band_w[:, offset + 1], source, preferred_eleme...  52.9 us
    dot_general x2, matrix products, body(): jnp.einsum('tqr,qc->trc', placed, received.reshape(-1, classes), preferre...  25.8 us
    ppermute x2, waiting for transfers between devices, with_halo(): lax.ppermute(lax.slice_in_dim(block, block.shape[dim] - width, None, axis...  15.6 us
    all_to_all x2, starting transfers between devices, fetch_blocks(): lax.all_to_all(blocks, 'node', split_axis=0, concat_axis=0, tiled=True)  15.4 us
    ppermute x2, starting transfers between devices, with_halo(): lax.ppermute(lax.slice_in_dim(block, 0, width, axis=dim), axis, backward)  14.3 us
    convert_element_type x2, other arithmetic, body(): fresh = jnp.where(seeded, clamped, scaled).astype(jnp.bfloat16)  12.1 us
    all_to_all x1, starting transfers between devices, body(): lax.all_to_all(far_block, 'node', split_axis=1, concat_axis=0, tiled=True)  11.2 us
    all_to_all x2, waiting for transfers between devices, fetch_blocks(): lax.all_to_all(blocks, 'node', split_axis=0, concat_axis=0, tiled=True)  11 us
  transfers between devices with their start and end apart: 7, of which 2 were waited for; matrix products, arithmetic and copies ran while one was open for 37% of the time, Pallas kernels for 0%

commit v1 on v0

v1 whole, which is shorter than its diff:
```python
import functools

import jax
import jax.numpy as jnp
from jax import lax
from jax.experimental import pallas as pl
from jax.experimental.pallas import tpu as pltpu
from jax.sharding import PartitionSpec as P

MESH = pl.DeviceIdType.MESH
BF = jnp.bfloat16
F32 = jnp.float32
STEP = 37
CHUNK = 16
LAG = 8


def rows_of(start, size):
    return pl.ds(pl.multiple_of(start, size), size)


def kernel(
    n, tiles, tile, classes, slots, blk,
    lab_hbm, bw_hbm, fw_hbm, fb_hbm, ft_hbm, fc_hbm, sm_hbm,
    out_hbm, res_ref,
    p0, p1, g32, acc, halo, send, recv, bw, fw, wp, wt, oh, dt, inv, outb, resb,
    fb, ft, fc, sm, req, qv, qs,
    load_sem, small_sem, req_ssem, req_rsem, q_sem, ssem, rsem, h_ssem, h_rsem, o_sem,
):
    me = lax.axis_index("node")
    nodes = tiles * tile
    pair = slots * blk
    wide = n * pair
    chunks = n // CHUNK
    kdim = CHUNK * pair

    def shift(p):
        return lax.rem(p * STEP, n)

    def source_of(p):
        return lax.rem(me + shift(p), n)

    def target_of(p):
        return lax.rem(me - shift(p) + n, n)

    barrier = pltpu.get_barrier_semaphore()

    def greet(i, carry):
        pl.semaphore_signal(barrier, inc=1, device_id=(lax.rem(me + i, n),), device_id_type=MESH)
        return carry

    lax.fori_loop(1, n, greet, 0)

    small = [
        pltpu.make_async_copy(src, dst, small_sem.at[i])
        for i, (src, dst) in enumerate(((fb_hbm, fb), (ft_hbm, ft), (fc_hbm, fc), (sm_hbm, sm)))
    ]
    large = [
        pltpu.make_async_copy(fw_hbm, fw, load_sem.at[0]),
        pltpu.make_async_copy(lab_hbm, p0.at[pl.ds(tile, nodes)], load_sem.at[1]),
        pltpu.make_async_copy(bw_hbm, bw, load_sem.at[2]),
    ]
    for copy in small + large:
        copy.start()
    for copy in small:
        copy.wait()

    lane = lax.broadcasted_iota(jnp.int32, (n, tile), 1)
    columns = [jnp.broadcast_to(fb[k : k + 1, :], (n, n)).T for k in range(slots)]
    table = jnp.where(lane == 0, columns[0], columns[1])
    for s in range(n):
        req[s] = table[s : s + 1]

    pl.semaphore_wait(barrier, n - 1)

    def ask(p, carry):
        s = source_of(p)
        pltpu.make_async_remote_copy(
            req.at[s], qv.at[p], req_ssem, req_rsem, device_id=(s,), device_id_type=MESH
        ).start()
        return carry

    lax.fori_loop(1, n, ask, 0)
    qv[0] = req[me]
    large[1].wait()

    nxt = lax.rem(me + 1, n)
    prv = lax.rem(me + n - 1, n)

    def halo_copies(it, cur):
        up = pltpu.make_async_remote_copy(
            cur.at[pl.ds(nodes, tile)], halo.at[it, 0], h_ssem.at[it, 0], h_rsem.at[it, 0],
            device_id=(nxt,), device_id_type=MESH,
        )
        down = pltpu.make_async_remote_copy(
            cur.at[pl.ds(tile, tile)], halo.at[it, 1], h_ssem.at[it, 1], h_rsem.at[it, 1],
            device_id=(prv,), device_id_type=MESH,
        )
        return up, down

    halo0 = halo_copies(0, p0)
    for copy in halo0:
        copy.start()

    def widen(t, carry):
        rows = p0[rows_of(tile + t * tile, tile), :].astype(F32)
        g32[rows_of(t * (tile // blk), tile // blk)] = rows.reshape(tile // blk, blk, classes)
        return carry

    lax.fori_loop(0, tiles, widen, 0)

    large[0].wait()

    def place(p, carry):
        wp[p] = fw[source_of(p)]
        return carry

    lax.fori_loop(0, n, place, 0)

    def turn(j, carry):
        part = wp[pl.ds(j * (tile // pair), tile // pair)].reshape(tile, tile)
        wt[:, rows_of(j * tile, tile)] = part.astype(F32).T.astype(BF)
        return carry

    lax.fori_loop(0, wide // tile, turn, 0)

    row8 = lax.broadcasted_iota(jnp.int32, (8, n), 0)
    number = [jnp.where(fc[...] > k, ft[k : k + 1, :], -1) for k in range(slots)]
    numbers = jnp.where(row8 == 0, number[0], number[1]).astype(F32).astype(BF)
    step = 512

    def mark(j, carry):
        col = lax.broadcasted_iota(jnp.int32, (n, step), 1) + j * step
        src = lax.rem(me + lax.rem((col // pair) * STEP, n), n)
        pick = jnp.where(lax.broadcasted_iota(jnp.int32, (n, step), 0) == src, 1.0, 0.0).astype(BF)
        found = jnp.dot(numbers, pick, preferred_element_type=F32)
        first = lax.rem(col[:1] // blk, slots) == 0
        mine = jnp.where(first, found[:1], found[1:2])
        ids = lax.broadcasted_iota(jnp.int32, (tiles, step), 0).astype(F32)
        oh[:, rows_of(j * step, step)] = jnp.where(mine == ids, 1.0, 0.0)
        return carry

    lax.fori_loop(0, wide // step, mark, 0)

    far_deg = jnp.dot(oh[...].astype(BF), wp[...].reshape(wide, tile), preferred_element_type=F32)
    seeds = sm[...].astype(F32)
    stack = jnp.concatenate([far_deg, seeds, jnp.zeros((tile - 2 * tiles, tile), F32)], axis=0)
    dt[...] = stack.T
    large[2].wait()

    def invert(t, carry):
        both = dt[...]
        far = jnp.sum(jnp.where(lane == t, both, 0.0), axis=1, keepdims=True)
        seed = jnp.sum(jnp.where(lane == t + tiles, both, 0.0), axis=1, keepdims=True)
        band = bw[t, 0].astype(F32) + bw[t, 1].astype(F32) + bw[t, 2].astype(F32)
        one = 1.0 / (jnp.sum(band, axis=1, keepdims=True) + far)
        inv[rows_of(t * tile, tile), :] = jnp.broadcast_to(jnp.where(seed > 0.5, -one, one), (tile, tile))
        return carry

    lax.fori_loop(0, tiles, invert, 0)

    asked = pltpu.make_async_remote_copy(
        req.at[pl.ds(1, n - 1)], qv.at[pl.ds(1, n - 1)], req_ssem, req_rsem,
        device_id=(nxt,), device_id_type=MESH,
    )
    asked.wait_recv()
    to_scalar = pltpu.make_async_copy(qv, qs, q_sem)
    to_scalar.start()
    to_scalar.wait()

    def exchange(it):
        def gather(p):
            blocks = [g32[qs[p, 0, k]] for k in range(slots)]
            return jnp.concatenate(blocks, axis=0).astype(BF)

        def ship(p):
            pltpu.make_async_remote_copy(
                send.at[it, p], recv.at[it, p], ssem.at[it], rsem.at[it, p // CHUNK],
                device_id=(target_of(p),), device_id_type=MESH,
            ).start()

        recv[it, 0] = gather(0)

        def first(p, carry):
            send[it, p] = gather(p)
            return carry

        lax.fori_loop(1, 1 + LAG, first, 0)

        def both(p, carry):
            send[it, p + LAG] = gather(p + LAG)
            ship(p)
            return carry

        lax.fori_loop(1, n - LAG, both, 0)

        def last(p, carry):
            ship(p)
            return carry

        lax.fori_loop(n - LAG, n, last, 0)

    def band(cur, t):
        lhs = jnp.concatenate([bw[t, 0], bw[t, 1], bw[t, 2]], axis=1)
        rhs = cur[pl.ds(pl.multiple_of(t * tile, tile), 3 * tile), :]
        acc[rows_of(t * tile, tile), :] = jnp.dot(lhs, rhs, preferred_element_type=F32)

    def band_all(it, cur, copies):
        def inner(t, carry):
            band(cur, t)
            return carry

        lax.fori_loop(1, tiles - 1, inner, 0)
        for copy in copies:
            copy.wait_recv()
        cur[pl.ds(0, tile), :] = halo[it, 0]
        cur[pl.ds(tile + nodes, tile), :] = halo[it, 1]
        band(cur, 0)
        band(cur, tiles - 1)

    group = 4

    def far(it):
        for c in range(chunks):
            low = 1 if c == 0 else 0
            span = pl.ds(c * CHUNK + low, CHUNK - low)
            pltpu.make_async_remote_copy(
                send.at[it, span], recv.at[it, span], ssem.at[it], rsem.at[it, c],
                device_id=(nxt,), device_id_type=MESH,
            ).wait_recv()

        def chunk(c, carry):
            rhs = recv[it, pl.ds(c * CHUNK, CHUNK)].reshape(kdim, classes)
            cols = rows_of(c * kdim, kdim)

            def some(g, inner):
                weights = wt[:, cols]
                parts = []
                for j in range(group):
                    keep = oh[pl.ds(g * group + j, 1), cols].astype(BF)
                    parts.append(weights * jnp.broadcast_to(keep, (tile, kdim)))
                lhs = jnp.concatenate(parts, axis=0)
                rows = rows_of(g * group * tile, group * tile)
                acc[rows, :] = acc[rows, :] + jnp.dot(lhs, rhs, preferred_element_type=F32)
                return inner

            lax.fori_loop(0, tiles // group, some, 0)
            return carry

        lax.fori_loop(0, chunks, chunk, 0)

    sub = 32

    def fresh(row):
        spread = acc[rows_of(row, sub), :]
        signed = inv[rows_of(row, sub), :]
        one = jnp.abs(signed)
        square = jnp.sum(spread * spread, axis=1, keepdims=True)
        mean = square * one * one * (1.0 / classes)
        factor = one / jnp.maximum(jnp.sqrt(mean), 0.05)
        reps = classes // tile
        scaled = spread * jnp.concatenate([factor] * reps, axis=1)
        seeded = jnp.concatenate([signed] * reps, axis=1) < 0.0
        given = p0[pl.ds(pl.multiple_of(tile + row, sub), sub), :].astype(F32)
        return jnp.where(seeded, given, scaled).astype(BF)

    def fold(change):
        total = jnp.sum(change, axis=0, keepdims=True)
        return sum(total[:, i * tile : (i + 1) * tile] for i in range(classes // tile))

    exchange(0)
    band_all(0, p0, halo0)
    far(0)

    def finish0(i, carry):
        row = i * sub
        new = fresh(row)
        p1[pl.ds(pl.multiple_of(tile + row, sub), sub), :] = new
        g32[pl.ds(i * (sub // blk), sub // blk)] = new.astype(F32).reshape(sub // blk, blk, classes)
        return carry

    lax.fori_loop(0, nodes // sub, finish0, 0)

    halo1 = halo_copies(1, p1)
    for copy in halo1:
        copy.start()
    exchange(1)

    def change0(t, carry):
        total = jnp.zeros((1, tile), F32)
        for j in range(tile // sub):
            rows = pl.ds(pl.multiple_of(tile + t * tile + j * sub, sub), sub)
            total = total + fold(jnp.abs(p1[rows, :].astype(F32) - p0[rows, :].astype(F32)))
        resb[0, pl.ds(t, 1), :] = total
        return carry

    lax.fori_loop(0, tiles, change0, 0)
    band_all(1, p1, halo1)
    far(1)

    def out_copy(t):
        rows = rows_of(t * tile, tile)
        return pltpu.make_async_copy(outb.at[rows], out_hbm.at[rows], o_sem)

    def finish1(t, carry):
        total = jnp.zeros((1, tile), F32)
        for j in range(tile // sub):
            row = t * tile + j * sub
            new = fresh(row)
            outb[rows_of(row, sub), :] = new
            old = p1[pl.ds(pl.multiple_of(tile + row, sub), sub), :].astype(F32)
            total = total + fold(jnp.abs(new.astype(F32) - old))
        resb[1, pl.ds(t, 1), :] = total

        @pl.when(t > 0)
        def _():
            out_copy(t - 1).start()

        return carry

    lax.fori_loop(0, tiles, finish1, 0)
    out_copy(tiles - 1).start()

    for it in range(2):
        block = jnp.concatenate([resb[it], jnp.zeros((tile - tiles, tile), F32)], axis=0)
        res_ref[it : it + 1, :] = jnp.sum(block.T, axis=0, keepdims=True)[:, :tiles]

    asked.wait_send()
    for copy in halo0 + halo1:
        copy.wait_send()
    for it in range(2):
        span = pl.ds(1, n - 1)
        pltpu.make_async_remote_copy(
            send.at[it, span], recv.at[it, span], ssem.at[it], rsem.at[it, 0],
            device_id=(nxt,), device_id_type=MESH,
        ).wait_send()
    pltpu.make_async_copy(outb, out_hbm, o_sem).wait()


def body(labels, seed_mask, band_w, far_block, far_tile, far_count, far_w):
    nodes, classes = labels.shape
    tiles, _, tile, _ = band_w.shape
    _, n, slots, blk, _ = far_w.shape
    any_space = pl.BlockSpec(memory_space=pl.ANY)
    vmem = pl.BlockSpec(memory_space=pltpu.VMEM)
    dma = pltpu.SemaphoreType.DMA
    wide = n * slots * blk
    final, residual = pl.pallas_call(
        functools.partial(kernel, n, tiles, tile, classes, slots, blk),
        out_shape=(
            jax.ShapeDtypeStruct((nodes, classes), BF),
            jax.ShapeDtypeStruct((2, tiles), F32),
        ),
        in_specs=[any_space] * 7,
        out_specs=(any_space, vmem),
        scratch_shapes=[
            pltpu.VMEM((nodes + 2 * tile, classes), BF),
            pltpu.VMEM((nodes + 2 * tile, classes), BF),
            pltpu.VMEM((nodes // blk, blk, classes), F32),
            pltpu.VMEM((nodes, classes), F32),
            pltpu.VMEM((2, 2, tile, classes), BF),
            pltpu.VMEM((2, n, slots * blk, classes), BF),
            pltpu.VMEM((2, n, slots * blk, classes), BF),
            pltpu.VMEM(band_w.shape, BF),
            pltpu.VMEM((n, slots * blk, tile), BF),
            pltpu.VMEM((n, slots * blk, tile), BF),
            pltpu.VMEM((tile, wide), BF),
            pltpu.VMEM((tiles, wide), F32),
            pltpu.VMEM((tile, tile), F32),
            pltpu.VMEM((nodes, tile), F32),
            pltpu.VMEM((nodes, classes), BF),
            pltpu.VMEM((2, tiles, tile), F32),
            pltpu.VMEM((slots, n), jnp.int32),
            pltpu.VMEM((slots, n), jnp.int32),
            pltpu.VMEM((1, n), jnp.int32),
            pltpu.VMEM((tiles, tile), jnp.int32),
            pltpu.VMEM((n, 1, tile), jnp.int32),
            pltpu.VMEM((n, 1, tile), jnp.int32),
            pltpu.SMEM((n, 1, tile), jnp.int32),
            dma((3,)),
            dma((4,)),
            dma,
            dma,
            dma,
            dma((2,)),
            dma((2, n // CHUNK)),
            dma((2, 2)),
            dma((2, 2)),
            dma,
        ],
        compiler_params=pltpu.CompilerParams(
            collective_id=0, has_side_effects=True, vmem_limit_bytes=62 * 2**20
        ),
    )(
        labels,
        band_w,
        far_w.reshape(n, slots * blk, tile),
        far_block[0].T,
        far_tile[0].T,
        far_count,
        seed_mask.reshape(tiles, tile),
    )
    return final, residual


def solution(mesh):
    placed = (
        P("node", None),
        P("node"),
        P("node", None, None, None),
        P("node", None, None),
        P("node", None, None),
        P("node", None),
        P("node", None, None, None, None),
    )
    return jax.shard_map(
        body,
        mesh=mesh,
        in_specs=placed,
        out_specs=(P("node", None), P(None, "node")),
        check_vma=False,
    )
```

time: 185 us -> 143 us (0.77)
  the two profiles are of different devices: /device:TPU:0 before, /device:TPU:1 now
where the time goes in v1:
time: 143 us
  Pallas kernels  138 us (97%)
  local copies, waits for them, and re-layouts  5.04 us (4%)
    pallas_call x1, Pallas kernels, body(): pl.pallas_call(functools.partial(kernel, n, tiles, tile, classes, slots,...  138 us
    unnamed x4, local copies, waits for them, and re-layouts  5.04 us

profile of v1, /device:TPU:1, one launch (start us, length us, event | category | flops | bytes accessed | tf_op | source)
XLA Modules:
  0.0 143.3 jit_solution(6607297426161174281)
XLA Ops:
  0.6 137.7 %shard_map.86 = (bf16[4096,512]{1,0:T(8,128)(2,1)}, f32[2,32]{1,0:T(2,128)}) custom-call(bf16[4096,512]{1,0:T(8,128)(2,1)} %lab_hbm.1, bf16[32,3,128,128]{3,2,1,0:T(8,128)(2,1)} %bw_hbm.1, bf16[128,16,128]{2,1,0:T(8,128)(2,1)} %bitcast.8, s32[2,128]{1,0:T(2,128)} %bitcast.10, s32[2,128]{1,0:T(2,128)} %bitcast.11, s32[1,128]{1,0:T(1,128)} %fc_hbm.1, ...), custom_call_target="tpu_custom_call" | custom-call | tf_op jit(solution)/shard_map/pallas_call | solution.py:348
  138.3 0.0 copy-start
  138.3 4.5 %copy.11 = bf16[4096,512]{1,0:T(8,128)(2,1)} copy(bf16[4096,512]{1,0:T(8,128)(2,1)} %get-tuple-element.4) | data formatting | bytes 8388608
  142.8 0.0 copy-done
  142.8 0.6 copy.12
Async XLA Ops:
  138.3 4.5 %copy-start = (f32[2,32]{1,0:T(2,128)S(1)}, f32[2,32]{1,0:T(2,128)}, u32[]{:S(2)}) copy-start(f32[2,32]{1,0:T(2,128)} %get-tuple-element.5) | copy-start | bytes 772

commit v2 on v1

v2 whole, which is shorter than its diff:
```python
import functools

import jax
import jax.numpy as jnp
from jax import lax
from jax.experimental import pallas as pl
from jax.experimental.pallas import tpu as pltpu
from jax.sharding import PartitionSpec as P

MESH = pl.DeviceIdType.MESH
BF = jnp.bfloat16
F32 = jnp.float32
STEP = 91
BACK = 83
CUTS = (0, 32, 64, 88, 112, 128)
RUN = 8


def rows_of(start, size):
    return pl.ds(pl.multiple_of(start, size), size)


def kernel(
    n, tiles, tile, classes, slots, blk,
    lab_hbm, bw_hbm, fw_hbm, fb_hbm, ft_hbm, fc_hbm, sm_hbm,
    out_ref, res_ref,
    p0, p1, g32, acc, halo, send, recv, bw, fw, wp, wt, oh, dt, inv, resb, sum0, sum1, fac0, fac1,
    fb, ft, fc, sm, req, qv, qs,
    load_sem, small_sem, req_ssem, req_rsem, q_sem, ssem, rsem, h_ssem, h_rsem,
):
    me = lax.axis_index("node")
    nodes = tiles * tile
    pair = slots * blk
    wide = n * pair
    sums, factors = (sum0, sum1), (fac0, fac1)
    chunks = len(CUTS) - 1

    def plus(a, b):
        return (a + b) & (n - 1)

    def source_of(p):
        return plus(me, p * STEP)

    def target_of(p):
        return plus(me, -p * STEP)

    def far_first(i):
        return i ^ 84

    def each_peer(step):
        lax.fori_loop(0, 84, step, 0)
        lax.fori_loop(85, n, step, 0)

    small = [
        pltpu.make_async_copy(src, dst, small_sem.at[i])
        for i, (src, dst) in enumerate(((fb_hbm, fb), (ft_hbm, ft), (fc_hbm, fc), (sm_hbm, sm)))
    ]
    large = [
        pltpu.make_async_copy(fw_hbm, fw, load_sem.at[0]),
        pltpu.make_async_copy(lab_hbm, p0.at[pl.ds(tile, nodes)], load_sem.at[1]),
        pltpu.make_async_copy(bw_hbm, bw, load_sem.at[2]),
    ]
    for copy in small + large:
        copy.start()
    barrier = pltpu.get_barrier_semaphore()

    def greet(i, carry):
        pl.semaphore_signal(
            barrier, inc=1, device_id=(plus(me, far_first(i)),), device_id_type=MESH
        )
        return carry

    with jax.named_scope("s_greet"):
        each_peer(greet)
    for copy in small:
        copy.wait()

    lane = lax.broadcasted_iota(jnp.int32, (n, tile), 1)
    columns = [jnp.broadcast_to(fb[k : k + 1, :], (n, n)).T for k in range(slots)]
    table = jnp.where(lane == 0, columns[0], columns[1])
    for s in range(n):
        req[s] = table[s : s + 1]

    with jax.named_scope("s_barrier"):
        pl.semaphore_wait(barrier, n - 1)

    def ask(i, carry):
        distance = far_first(i)
        s = plus(me, distance)
        pltpu.make_async_remote_copy(
            req.at[s], qv.at[(distance * BACK) & (n - 1)], req_ssem, req_rsem,
            device_id=(s,), device_id_type=MESH,
        ).start()
        return carry

    with jax.named_scope("s_ask"):
        each_peer(ask)
    qv[0] = req[me]
    large[1].wait()

    nxt = plus(me, 1)
    prv = plus(me, n - 1)

    def halo_copies(it, cur):
        up = pltpu.make_async_remote_copy(
            cur.at[pl.ds(nodes, tile)], halo.at[it, 0], h_ssem.at[it, 0], h_rsem.at[it, 0],
            device_id=(nxt,), device_id_type=MESH,
        )
        down = pltpu.make_async_remote_copy(
            cur.at[pl.ds(tile, tile)], halo.at[it, 1], h_ssem.at[it, 1], h_rsem.at[it, 1],
            device_id=(prv,), device_id_type=MESH,
        )
        return up, down

    halo0 = halo_copies(0, p0)
    for copy in halo0:
        copy.start()

    def widen(t, carry):
        rows = p0[rows_of(tile + t * tile, tile), :].astype(F32)
        g32[rows_of(t * (tile // blk), tile // blk)] = rows.reshape(tile // blk, blk, classes)
        return carry

    lax.fori_loop(0, tiles, widen, 0)
    edge = jnp.zeros((tile, classes), BF)
    for ref in (p0, p1):
        ref[pl.ds(0, tile), :] = edge
        ref[pl.ds(tile + nodes, tile), :] = edge

    large[0].wait()

    def place(p, carry):
        wp[p] = fw[source_of(p)]
        return carry

    lax.fori_loop(0, n, place, 0)

    def turn(j, carry):
        part = wp[pl.ds(j * (tile // pair), tile // pair)].reshape(tile, tile)
        wt[:, rows_of(j * tile, tile)] = part.astype(F32).T.astype(BF)
        return carry

    lax.fori_loop(0, wide // tile, turn, 0)

    row8 = lax.broadcasted_iota(jnp.int32, (8, n), 0)
    number = [jnp.where(fc[...] > k, ft[k : k + 1, :], -1) for k in range(slots)]
    numbers = jnp.where(row8 == 0, number[0], number[1]).astype(F32).astype(BF)
    step = 512

    def mark(j, carry):
        col = lax.broadcasted_iota(jnp.int32, (n, step), 1) + j * step
        src = (me + (col // pair) * STEP) & (n - 1)
        pick = jnp.where(lax.broadcasted_iota(jnp.int32, (n, step), 0) == src, 1.0, 0.0).astype(BF)
        found = jnp.dot(numbers, pick, preferred_element_type=F32)
        first = lax.rem(col[:1] // blk, slots) == 0
        mine = jnp.where(first, found[:1], found[1:2])
        ids = lax.broadcasted_iota(jnp.int32, (tiles, step), 0).astype(F32)
        oh[:, rows_of(j * step, step)] = jnp.where(mine == ids, 1.0, 0.0)
        return carry

    lax.fori_loop(0, wide // step, mark, 0)

    far_deg = jnp.dot(oh[...].astype(BF), wp[...].reshape(wide, tile), preferred_element_type=F32)
    seeds = sm[...].astype(F32)
    stack = jnp.concatenate([far_deg, seeds, jnp.zeros((tile - 2 * tiles, tile), F32)], axis=0)
    dt[...] = stack.T
    large[2].wait()

    def invert(i, carry):
        both = dt[...]
        for k in range(4):
            t = i * 4 + k
            far = jnp.sum(jnp.where(lane == t, both, 0.0), axis=1, keepdims=True)
            seed = jnp.sum(jnp.where(lane == t + tiles, both, 0.0), axis=1, keepdims=True)
            weight = bw[t, 0].astype(F32) + bw[t, 1].astype(F32) + bw[t, 2].astype(F32)
            one = 1.0 / (jnp.sum(weight, axis=1, keepdims=True) + far)
            inv[rows_of(t * tile, tile), :] = jnp.broadcast_to(jnp.where(seed > 0.5, -one, one), (tile, tile))
        return carry

    with jax.named_scope("s_invert"):
        lax.fori_loop(0, tiles // 4, invert, 0)

    asked = pltpu.make_async_remote_copy(
        req.at[pl.ds(1, n - 1)], qv.at[pl.ds(1, n - 1)], req_ssem, req_rsem,
        device_id=(nxt,), device_id_type=MESH,
    )
    with jax.named_scope("s_waitreq"):
        asked.wait_recv()
    def to_scalar(g):
        span = pl.ds(g * RUN, RUN)
        return pltpu.make_async_copy(qv.at[span], qs.at[span], q_sem.at[g])

    runs = n // RUN
    for g in range(runs):
        to_scalar(g).start()

    def exchange(it):
        def gather(p):
            blocks = [g32[qs[p, 0, k]] for k in range(slots)]
            return jnp.concatenate(blocks, axis=0).astype(BF)

        def load(g, low=0):
            if it == 0:
                to_scalar(g).wait()
            for j in range(low, RUN):
                send[it, g * RUN + j] = gather(g * RUN + j)

        def ship(g, low=0):
            c = sum((g >= cut // RUN).astype(jnp.int32) for cut in CUTS[1:-1])
            for j in range(low, RUN):
                p = g * RUN + j
                pltpu.make_async_remote_copy(
                    send.at[it, p], recv.at[it, p], ssem.at[it], rsem.at[it, c],
                    device_id=(target_of(p),), device_id_type=MESH,
                ).start()

        def both(g, carry):
            load(g)
            ship(g - 1)
            return carry

        zero = jnp.int32(0)
        load(zero, 1)
        recv[it, 0] = gather(0)
        load(zero + 1)
        ship(zero, 1)
        lax.fori_loop(2, runs, both, 0)
        ship(zero + (runs - 1))

    def band(cur, t):
        lhs = jnp.concatenate([bw[t, 0], bw[t, 1], bw[t, 2]], axis=1)
        rhs = cur[pl.ds(pl.multiple_of(t * tile, tile), 3 * tile), :]
        acc[rows_of(t * tile, tile), :] = jnp.dot(lhs, rhs, preferred_element_type=F32)

    def band_all(cur):
        def inner(i, carry):
            band(cur, 2 * i)
            band(cur, 2 * i + 1)
            return carry

        lax.fori_loop(0, tiles // 2, inner, 0)

    def edges(it, copies):
        for copy in copies:
            copy.wait_recv()
        for side, t, o in ((0, 0, 0), (1, tiles - 1, 2)):
            rows = pl.ds(t * tile, tile)
            acc[rows, :] = acc[rows, :] + jnp.dot(bw[t, o], halo[it, side], preferred_element_type=F32)

    def arrived(it, c):
        low, high = max(CUTS[c], 1), CUTS[c + 1]
        span = pl.ds(low, high - low)
        pltpu.make_async_remote_copy(
            send.at[it, span], recv.at[it, span], ssem.at[it], rsem.at[it, c],
            device_id=(nxt,), device_id_type=MESH,
        ).wait_recv()

    def product(it, c, t, count):
        low, size = CUTS[c], CUTS[c + 1] - CUTS[c]
        cols = pl.ds(low * pair, size * pair)
        rhs = recv[it, pl.ds(low, size)].reshape(size * pair, classes)
        weights = wt[:, cols]
        parts = []
        for j in range(count):
            keep = oh[pl.ds(t + j, 1), cols].astype(BF)
            parts.append(weights * jnp.broadcast_to(keep, (tile, size * pair)))
        lhs = jnp.concatenate(parts, axis=0)
        return jnp.dot(lhs, rhs, preferred_element_type=F32)

    group = 4

    def far(it, copies):
        for c in range(chunks - 1):
            with jax.named_scope(f"s_wait{c}"):
                arrived(it, c)

            def some(g, carry, c=c):
                rows = rows_of(g * group * tile, group * tile)
                acc[rows, :] = acc[rows, :] + product(it, c, g * group, group)
                return carry

            with jax.named_scope(f"s_mm{c}"):
                lax.fori_loop(0, tiles // group, some, 0)
        edges(it, copies)
        with jax.named_scope("s_waitlast"):
            arrived(it, chunks - 1)

    sub = 32
    reps = classes // tile

    def scale(it, t, slot):
        spread = acc[rows_of(t * tile, tile), :] + product(it, chunks - 1, t, 1)
        sums[slot][...] = spread
        one = jnp.abs(inv[rows_of(t * tile, tile), :])
        square = jnp.sum(spread * spread, axis=1, keepdims=True)
        mean = square * one * one * (1.0 / classes)
        factors[slot][...] = one / jnp.maximum(jnp.sqrt(mean), 0.05)

    def fresh(t, slot, j):
        part = pl.ds(j * sub, sub)
        row = t * tile + j * sub
        scaled = sums[slot][part, :] * jnp.concatenate([factors[slot][part, :]] * reps, axis=1)
        seeded = jnp.concatenate([inv[rows_of(row, sub), :]] * reps, axis=1) < 0.0
        given = p0[pl.ds(pl.multiple_of(tile + row, sub), sub), :].astype(F32)
        return jnp.where(seeded, given, scaled)

    def fold(change):
        total = jnp.sum(change.reshape(sub // 8, 8, classes), axis=0)
        return sum(total[:, i * tile : (i + 1) * tile] for i in range(reps))

    def finish(it, write):
        def step(i, carry):
            t = 2 * i
            scale(it, t + 1, 1)
            write(t, 0)
            scale(it, t + 2, 0)
            write(t + 1, 1)
            return carry

        last = jnp.int32(tiles - 1)
        scale(it, jnp.int32(0), 0)
        lax.fori_loop(0, tiles // 2 - 1, step, 0)
        scale(it, last, 1)
        write(last - 1, 0)
        write(last, 1)

    with jax.named_scope("s_exchange0"):
        exchange(0)
    with jax.named_scope("s_band0"):
        band_all(p0)
    far(0, halo0)

    def write0(t, slot):
        for j in range(tile // sub):
            new = fresh(t, slot, j)
            g32[pl.ds(t * (tile // blk) + j * (sub // blk), sub // blk)] = new.reshape(sub // blk, blk, classes)
            p1[pl.ds(pl.multiple_of(tile + t * tile + j * sub, sub), sub), :] = new.astype(BF)

    with jax.named_scope("s_finish0"):
        finish(0, write0)

    halo1 = halo_copies(1, p1)
    for copy in halo1:
        copy.start()
    with jax.named_scope("s_exchange1"):
        exchange(1)

    def change0(t, carry):
        total = jnp.zeros((8, tile), F32)
        for j in range(tile // sub):
            rows = pl.ds(pl.multiple_of(tile + t * tile + j * sub, sub), sub)
            total = total + fold(jnp.abs(p1[rows, :].astype(F32) - p0[rows, :].astype(F32)))
        resb[0, t] = total
        return carry

    with jax.named_scope("s_change0"):
        lax.fori_loop(0, tiles, change0, 0)
    with jax.named_scope("s_band1"):
        band_all(p1)
    far(1, halo1)

    def write1(t, slot):
        total = jnp.zeros((8, tile), F32)
        for j in range(tile // sub):
            row = t * tile + j * sub
            new = fresh(t, slot, j).astype(BF)
            out_ref[rows_of(row, sub), :] = new
            old = p1[pl.ds(pl.multiple_of(tile + row, sub), sub), :].astype(F32)
            total = total + fold(jnp.abs(new.astype(F32) - old))
        resb[1, t] = total

    with jax.named_scope("s_finish1"):
        finish(1, write1)

    with jax.named_scope("s_res"):
        for it in range(2):
            block = jnp.concatenate([jnp.sum(resb[it], axis=1), jnp.zeros((tile - tiles, tile), F32)], axis=0)
            res_ref[it : it + 1, :] = jnp.sum(block.T, axis=0, keepdims=True)[:, :tiles]

    asked.wait_send()
    for copy in halo0 + halo1:
        copy.wait_send()
    for it in range(2):
        span = pl.ds(1, n - 1)
        pltpu.make_async_remote_copy(
            send.at[it, span], recv.at[it, span], ssem.at[it], rsem.at[it, 0],
            device_id=(nxt,), device_id_type=MESH,
        ).wait_send()


def body(labels, seed_mask, band_w, far_block, far_tile, far_count, far_w):
    nodes, classes = labels.shape
    tiles, _, tile, _ = band_w.shape
    _, n, slots, blk, _ = far_w.shape
    hbm = pl.BlockSpec(memory_space=pltpu.HBM)
    vmem = pl.BlockSpec(memory_space=pltpu.VMEM)
    dma = pltpu.SemaphoreType.DMA
    wide = n * slots * blk
    final, residual = pl.pallas_call(
        functools.partial(kernel, n, tiles, tile, classes, slots, blk),
        out_shape=(
            pltpu.VMEM((nodes, classes), BF),
            pltpu.VMEM((2, tiles), F32),
        ),
        in_specs=[hbm] * 7,
        out_specs=(vmem, vmem),
        scratch_shapes=[
            pltpu.VMEM((nodes + 2 * tile, classes), BF),
            pltpu.VMEM((nodes + 2 * tile, classes), BF),
            pltpu.VMEM((nodes // blk, blk, classes), F32),
            pltpu.VMEM((nodes, classes), F32),
            pltpu.VMEM((2, 2, tile, classes), BF),
            pltpu.VMEM((2, n, slots * blk, classes), BF),
            pltpu.VMEM((2, n, slots * blk, classes), BF),
            pltpu.VMEM(band_w.shape, BF),
            pltpu.VMEM((n, slots * blk, tile), BF),
            pltpu.VMEM((n, slots * blk, tile), BF),
            pltpu.VMEM((tile, wide), BF),
            pltpu.VMEM((tiles, wide), F32),
            pltpu.VMEM((tile, tile), F32),
            pltpu.VMEM((nodes, tile), F32),
                pltpu.VMEM((2, tiles, 8, tile), F32),
            pltpu.VMEM((tile, classes), F32),
            pltpu.VMEM((tile, classes), F32),
            pltpu.VMEM((tile, tile), F32),
            pltpu.VMEM((tile, tile), F32),
            pltpu.VMEM((slots, n), jnp.int32),
            pltpu.VMEM((slots, n), jnp.int32),
            pltpu.VMEM((1, n), jnp.int32),
            pltpu.VMEM((tiles, tile), jnp.int32),
            pltpu.VMEM((n, 1, tile), jnp.int32),
            pltpu.VMEM((n, 1, tile), jnp.int32),
            pltpu.SMEM((n, 1, tile), jnp.int32),
            dma((3,)),
            dma((4,)),
            dma,
            dma,
            dma((n // RUN,)),
            dma((2,)),
            dma((2, len(CUTS) - 1)),
            dma((2, 2)),
            dma((2, 2)),
        ],
        compiler_params=pltpu.CompilerParams(
            collective_id=0, has_side_effects=True, vmem_limit_bytes=50 * 2**20
        ),
    )(
        *(
            pltpu.with_memory_space_constraint(x, pltpu.HBM)
            for x in (
                labels,
                band_w,
                far_w.reshape(n, slots * blk, tile),
                far_block[0].T,
                far_tile[0].T,
                far_count,
                seed_mask.reshape(tiles, tile),
            )
        )
    )
    return final, residual


def solution(mesh):
    placed = (
        P("node", None),
        P("node"),
        P("node", None, None, None),
        P("node", None, None),
        P("node", None, None),
        P("node", None),
        P("node", None, None, None, None),
    )
    return jax.shard_map(
        body,
        mesh=mesh,
        in_specs=placed,
        out_specs=(P("node", None), P(None, "node")),
        check_vma=False,
    )
```

time: 143 us -> 99.6 us (0.70)
  the two profiles are of different devices: /device:TPU:1 before, /device:TPU:6 now
where the time goes in v2:
time: 99.6 us; the launch traced here: 99.5 us
  Pallas kernels  96.3 us (97%)
  local copies, waits for them, and re-layouts  2.58 us (3%)
    pallas_call x1, Pallas kernels, body(): pl.pallas_call(functools.partial(kernel, n, tiles, tile, classes, slots,...  96.3 us
    unnamed x2, local copies, waits for them, and re-layouts  2.58 us

profile of v2, /device:TPU:6, one launch (start us, length us, event | category | flops | bytes accessed | tf_op | source)
XLA Modules:
  0.0 99.5 jit_solution(10646212987920443123)
XLA Ops:
  0.6 96.3 %shard_map.86 = (bf16[4096,512]{1,0:T(8,128)(2,1)S(1)}, f32[2,32]{1,0:T(2,128)S(1)}) custom-call(bf16[4096,512]{1,0:T(8,128)(2,1)} %lab_hbm.1, bf16[32,3,128,128]{3,2,1,0:T(8,128)(2,1)} %bw_hbm.1, bf16[128,16,128]{2,1,0:T(8,128)(2,1)} %bitcast.8, s32[2,128]{1,0:T(2,128)} %bitcast.10, s32[2,128]{1,0:T(2,128)} %bitcast.11, s32[1,128]{1,0:T(1,128)} %fc_hbm.1, ...), custom_call_target="tpu_custom_call" | custom-call | tf_op jit(solution)/shard_map/pallas_call | solution.py:399
  96.9 2.0 %copy.11 = bf16[4096,512]{1,0:T(8,128)(2,1)} copy(bf16[4096,512]{1,0:T(8,128)(2,1)S(1)} %get-tuple-element.2) | data formatting | bytes 8388608
  98.9 0.6 copy.12

commit v3 on v2

v3 whole, which is shorter than its diff:
```python
import functools

import jax
import jax.numpy as jnp
from jax import lax
from jax.experimental import pallas as pl
from jax.experimental.pallas import tpu as pltpu
from jax.sharding import PartitionSpec as P

MESH = pl.DeviceIdType.MESH
BF = jnp.bfloat16
F32 = jnp.float32
STEP = 91
BACK = 83
CHUNK = 16
FLOOR = 0.05
RUN = 8


def rows_of(start, size):
    return pl.ds(pl.multiple_of(start, size), size)


def fold_rows(change):
    rows, classes = change.shape
    total = jnp.sum(change.reshape(rows // 8, 8, classes), axis=0)
    return sum(total[:, i : i + 128] for i in range(0, classes, 128))


def close(tiles, tile, sub, new, old, first, out_hbm, res_hbm, second, res, copy_sem, res_sem):
    copy = pltpu.make_async_copy(new, out_hbm, copy_sem)
    copy.start()

    def change(t, carry):
        total = jnp.zeros((8, tile), F32)
        for j in range(tile // sub):
            low = t * tile + j * sub
            after = new[rows_of(low, sub), :].astype(F32)
            before = old[pl.ds(pl.multiple_of(tile + low, sub), sub), :].astype(F32)
            total = total + fold_rows(jnp.abs(after - before))
        second[t] = total
        return carry

    lax.fori_loop(0, tiles, change, 0)
    for it, part in enumerate((first, second)):
        block = jnp.concatenate([jnp.sum(part[...], axis=1), jnp.zeros((tile - tiles, tile), F32)], axis=0)
        res[it : it + 1, :] = jnp.sum(block.T, axis=0, keepdims=True)[:, :tiles]
    small = pltpu.make_async_copy(res, res_hbm, res_sem)
    small.start()
    small.wait()
    copy.wait()


def kernel(
    n, tiles, tile, classes, slots, blk,
    lab_hbm, bw_hbm, fw_hbm, fb_hbm, ft_hbm, fc_hbm, sm_hbm,
    out_ref, p1, resb,
    p0, g32, acc, halo, send, recv, bw, fw, wp, wt, mask, oh, dt, inv, sum0, sum1, sum2, sum3, fac0, fac1, fac2, fac3,
    fb, ft, fc, sm, req, qv, qs,
    load_sem, small_sem, req_ssem, req_rsem, q_sem, ssem, rsem, h_ssem, h_rsem,
):
    me = lax.axis_index("node")
    nodes = tiles * tile
    pair = slots * blk
    wide = n * pair
    sums, factors = (sum0, sum1, sum2, sum3), (fac0, fac1, fac2, fac3)
    chunks = n // CHUNK
    kdim = CHUNK * pair

    def plus(a, b):
        return (a + b) & (n - 1)

    def source_of(p):
        return plus(me, p * STEP)

    def target_of(p):
        return plus(me, -p * STEP)

    def far_first(i):
        return i ^ 84

    def each_peer(step):
        lax.fori_loop(0, 84, step, 0)
        lax.fori_loop(85, n, step, 0)

    small = [
        pltpu.make_async_copy(src, dst, small_sem.at[i])
        for i, (src, dst) in enumerate(((fb_hbm, fb), (ft_hbm, ft), (fc_hbm, fc), (sm_hbm, sm)))
    ]
    large = [
        pltpu.make_async_copy(fw_hbm, fw, load_sem.at[0]),
        pltpu.make_async_copy(lab_hbm, p0.at[pl.ds(tile, nodes)], load_sem.at[1]),
        pltpu.make_async_copy(bw_hbm, bw, load_sem.at[2]),
    ]
    for copy in small + large:
        copy.start()
    barrier = pltpu.get_barrier_semaphore()

    def greet(i, carry):
        pl.semaphore_signal(
            barrier, inc=1, device_id=(plus(me, far_first(i)),), device_id_type=MESH
        )
        return carry

    with jax.named_scope("s_greet"):
        each_peer(greet)
    for copy in small:
        copy.wait()

    lane = lax.broadcasted_iota(jnp.int32, (n, tile), 1)
    columns = [jnp.broadcast_to(fb[k : k + 1, :], (n, n)).T for k in range(slots)]
    table = jnp.where(lane == 0, columns[0], columns[1])
    for s in range(n):
        req[s] = table[s : s + 1]

    with jax.named_scope("s_barrier"):
        pl.semaphore_wait(barrier, n - 1)

    def ask(i, carry):
        distance = far_first(i)
        s = plus(me, distance)
        pltpu.make_async_remote_copy(
            req.at[s], qv.at[(distance * BACK) & (n - 1)], req_ssem, req_rsem,
            device_id=(s,), device_id_type=MESH,
        ).start()
        return carry

    with jax.named_scope("s_ask"):
        each_peer(ask)
    qv[0] = req[me]
    large[1].wait()

    nxt = plus(me, 1)
    prv = plus(me, n - 1)

    def halo_copies(it, cur, low=0, size=tile):
        part = pl.ds(low, size)
        up = pltpu.make_async_remote_copy(
            cur.at[pl.ds(nodes + low, size)], halo.at[it, 0, part], h_ssem.at[it, 0], h_rsem.at[it, 0],
            device_id=(nxt,), device_id_type=MESH,
        )
        down = pltpu.make_async_remote_copy(
            cur.at[pl.ds(tile + low, size)], halo.at[it, 1, part], h_ssem.at[it, 1], h_rsem.at[it, 1],
            device_id=(prv,), device_id_type=MESH,
        )
        return up, down

    halo0 = halo_copies(0, p0)
    for copy in halo0:
        copy.start()

    def widen(t, carry):
        rows = p0[rows_of(tile + t * tile, tile), :].astype(F32)
        g32[rows_of(t * (tile // blk), tile // blk)] = rows.reshape(tile // blk, blk, classes)
        return carry

    lax.fori_loop(0, tiles, widen, 0)
    edge = jnp.zeros((tile, classes), BF)
    for ref in (p0, p1):
        ref[pl.ds(0, tile), :] = edge
        ref[pl.ds(tile + nodes, tile), :] = edge

    large[0].wait()

    def place(p, carry):
        wp[p] = fw[source_of(p)]
        return carry

    lax.fori_loop(0, n, place, 0)

    def turn(j):
        part = wp[pl.ds(j * (tile // pair), tile // pair)].reshape(tile, tile)
        return part.astype(F32).T.astype(BF)

    def turn_chunk(c, carry):
        wt[c] = jnp.concatenate([turn(c * (kdim // tile) + j) for j in range(kdim // tile)], axis=1)
        return carry

    lax.fori_loop(0, chunks, turn_chunk, 0)

    row8 = lax.broadcasted_iota(jnp.int32, (8, n), 0)
    number = [jnp.where(fc[...] > k, ft[k : k + 1, :], -1) for k in range(slots)]
    numbers = jnp.where(row8 == 0, number[0], number[1]).astype(F32).astype(BF)
    step = 512

    def mark(j, carry):
        col = lax.broadcasted_iota(jnp.int32, (n, step), 1) + j * step
        src = (me + (col // pair) * STEP) & (n - 1)
        pick = jnp.where(lax.broadcasted_iota(jnp.int32, (n, step), 0) == src, 1.0, 0.0).astype(BF)
        found = jnp.dot(numbers, pick, preferred_element_type=F32)
        first = lax.rem(col[:1] // blk, slots) == 0
        mine = jnp.where(first, found[:1], found[1:2])
        ids = lax.broadcasted_iota(jnp.int32, (tiles, step), 0).astype(F32)
        oh[:, rows_of(j * step, step)] = jnp.where(mine == ids, 1.0, 0.0)
        return carry

    lax.fori_loop(0, wide // step, mark, 0)

    far_deg = jnp.dot(oh[...].astype(BF), wp[...].reshape(wide, tile), preferred_element_type=F32)
    seeds = sm[...].astype(F32)
    stack = jnp.concatenate([far_deg, seeds, jnp.zeros((tile - 2 * tiles, tile), F32)], axis=0)
    dt[...] = stack.T
    asked = pltpu.make_async_remote_copy(
        req.at[pl.ds(1, n - 1)], qv.at[pl.ds(1, n - 1)], req_ssem, req_rsem,
        device_id=(nxt,), device_id_type=MESH,
    )
    with jax.named_scope("s_waitreq"):
        asked.wait_recv()
    def to_scalar(g):
        span = pl.ds(g * RUN, RUN)
        return pltpu.make_async_copy(qv.at[span], qs.at[span], q_sem.at[g])

    runs = n // RUN
    for g in range(runs):
        to_scalar(g).start()

    def exchange(it):
        def gather(p):
            blocks = [g32[qs[p, 0, k]] for k in range(slots)]
            return jnp.concatenate(blocks, axis=0).astype(BF)

        def load(g, low=0):
            if it == 0:
                to_scalar(g).wait()
            for j in range(low, RUN):
                send[it, g * RUN + j] = gather(g * RUN + j)

        def ship(g, low=0):
            c = g // (CHUNK // RUN)
            for j in range(low, RUN):
                p = g * RUN + j
                pltpu.make_async_remote_copy(
                    send.at[it, p], recv.at[it, p], ssem.at[it], rsem.at[it, c],
                    device_id=(target_of(p),), device_id_type=MESH,
                ).start()

        def both(g, carry):
            load(g)
            ship(g - 1)
            if it == 1:
                low = pl.multiple_of((g // 2 - 1) * 16, 16)

                @pl.when(g % 2 == 0)
                def _():
                    for copy in halo_copies(1, p1, low, 16):
                        copy.start()

            return carry

        zero = jnp.int32(0)
        load(zero, 1)
        recv[it, 0] = gather(0)
        load(zero + 1)
        ship(zero, 1)
        lax.fori_loop(2, runs, both, 0)
        ship(zero + (runs - 1))
        if it == 1:
            for copy in halo_copies(1, p1, tile - 16, 16):
                copy.start()

    def band(cur, t):
        lhs = jnp.concatenate([bw[t, 0], bw[t, 1], bw[t, 2]], axis=1)
        rhs = cur[pl.ds(pl.multiple_of(t * tile, tile), 3 * tile), :]
        acc[rows_of(t * tile, tile), :] = jnp.dot(lhs, rhs, preferred_element_type=F32)

    def band_all(cur):
        def inner(i, carry):
            band(cur, 2 * i)
            band(cur, 2 * i + 1)
            return carry

        lax.fori_loop(0, tiles // 2, inner, 0)

    def edges(it, copies):
        for copy in copies:
            copy.wait_recv()
        for side, t, o in ((0, 0, 0), (1, tiles - 1, 2)):
            rows = pl.ds(t * tile, tile)
            acc[rows, :] = acc[rows, :] + jnp.dot(bw[t, o], halo[it, side], preferred_element_type=F32)

    def arrived(it, c, low=0):
        span = pl.ds(c * CHUNK + low, CHUNK - low)
        pltpu.make_async_remote_copy(
            send.at[it, span], recv.at[it, span], ssem.at[it], rsem.at[it, c],
            device_id=(nxt,), device_id_type=MESH,
        ).wait_recv()

    def product(it, c, t, count):
        rhs = recv[it, pl.ds(c * CHUNK, CHUNK)].reshape(kdim, classes)
        weights = wt[c].reshape(tile // 16, 16, kdim)
        parts = [(weights * mask[c, t + j][None]).reshape(tile, kdim) for j in range(count)]
        lhs = parts[0] if count == 1 else jnp.concatenate(parts, axis=0)
        return jnp.dot(lhs, rhs, preferred_element_type=F32)

    group = 16

    def far(it, copies):
        def chunk(c, carry):
            with jax.named_scope("s_wait"):
                arrived(it, c)
            multiply(c)
            return carry

        def multiply(c):
            def some(g, inner):
                rows = rows_of(g * group * tile, group * tile)
                acc[rows, :] = acc[rows, :] + product(it, c, g * group, group)
                return inner

            with jax.named_scope("s_mm"):
                lax.fori_loop(0, tiles // group, some, 0)

        arrived(it, 0, 1)
        multiply(jnp.int32(0))
        lax.fori_loop(1, chunks - 1, chunk, 0)
        edges(it, copies)
        with jax.named_scope("s_waitlast"):
            arrived(it, chunks - 1)

    sub = 32
    reps = classes // tile

    def scale(it, t, slot):
        spread = acc[rows_of(t * tile, tile), :] + product(it, chunks - 1, t, 1)
        sums[slot][...] = spread
        one = jnp.abs(inv[rows_of(t * tile, tile), :])
        square = jnp.sum(spread * spread, axis=1, keepdims=True)
        mean = square * one * one * (1.0 / classes)
        factors[slot][...] = one * lax.rsqrt(jnp.maximum(mean, FLOOR * FLOOR))

    def fresh(t, slot, j):
        part = pl.ds(j * sub, sub)
        row = t * tile + j * sub
        scaled = sums[slot][part, :] * jnp.concatenate([factors[slot][part, :]] * reps, axis=1)
        seeded = jnp.concatenate([inv[rows_of(row, sub), :]] * reps, axis=1) < 0.0
        given = p0[pl.ds(pl.multiple_of(tile + row, sub), sub), :].astype(F32)
        return jnp.where(seeded, given, scaled)

    fold = fold_rows

    def finish(it, write):
        def step(i, carry):
            t = 4 * i
            scale(it, t + 2, 2)
            scale(it, t + 3, 3)
            write(t, 0)
            write(t + 1, 1)
            scale(it, t + 4, 0)
            scale(it, t + 5, 1)
            write(t + 2, 2)
            write(t + 3, 3)
            return carry

        last = jnp.int32(tiles - 4)
        scale(it, jnp.int32(0), 0)
        scale(it, jnp.int32(1), 1)
        lax.fori_loop(0, tiles // 4 - 1, step, 0)
        scale(it, last + 2, 2)
        scale(it, last + 3, 3)
        for j in range(4):
            write(last + j, j)

    with jax.named_scope("s_exchange0"):
        exchange(0)

    large[2].wait()

    def invert(i, carry):
        both = dt[...]
        for k in range(4):
            t = i * 4 + k
            far = jnp.sum(jnp.where(lane == t, both, 0.0), axis=1, keepdims=True)
            seed = jnp.sum(jnp.where(lane == t + tiles, both, 0.0), axis=1, keepdims=True)
            weight = bw[t, 0].astype(F32) + bw[t, 1].astype(F32) + bw[t, 2].astype(F32)
            one = 1.0 / (jnp.sum(weight, axis=1, keepdims=True) + far)
            inv[rows_of(t * tile, tile), :] = jnp.broadcast_to(jnp.where(seed > 0.5, -one, one), (tile, tile))
        return carry

    with jax.named_scope("s_invert"):
        lax.fori_loop(0, tiles // 4, invert, 0)

    def spread_mask(c, carry):
        def some(i, inner):
            rows = oh[rows_of(i * 8, 8), rows_of(c * kdim, kdim)]
            for j in range(8):
                mask[c, i * 8 + j] = jnp.broadcast_to(rows[j : j + 1], (16, kdim)).astype(BF)
            return inner

        lax.fori_loop(0, tiles // 8, some, 0)
        return carry

    with jax.named_scope("s_mask"):
        lax.fori_loop(0, chunks, spread_mask, 0)
    with jax.named_scope("s_band0"):
        band_all(p0)
    far(0, halo0)

    def write0(t, slot):
        for j in range(tile // sub):
            new = fresh(t, slot, j)
            g32[pl.ds(t * (tile // blk) + j * (sub // blk), sub // blk)] = new.reshape(sub // blk, blk, classes)

    with jax.named_scope("s_finish0"):
        finish(0, write0)

    def narrow(t):
        new = g32[rows_of(t * (tile // blk), tile // blk)].reshape(tile, classes).astype(BF)
        p1[rows_of(tile + t * tile, tile), :] = new

    narrow(jnp.int32(0))
    narrow(jnp.int32(tiles - 1))

    halo1 = halo_copies(1, p1)
    with jax.named_scope("s_exchange1"):
        exchange(1)

    def change0(t, carry):
        total = jnp.zeros((8, tile), F32)
        for j in range(tile // sub):
            rows = pl.ds(pl.multiple_of(tile + t * tile + j * sub, sub), sub)
            part = pl.ds(t * (tile // blk) + j * (sub // blk), sub // blk)
            new = g32[part].reshape(sub, classes).astype(BF)
            p1[rows, :] = new
            total = total + fold(jnp.abs(new.astype(F32) - p0[rows, :].astype(F32)))
        resb[t] = total
        return carry

    def edge_change(t):
        total = jnp.zeros((8, tile), F32)
        for j in range(tile // sub):
            rows = pl.ds(tile + t * tile + j * sub, sub)
            total = total + fold(jnp.abs(p1[rows, :].astype(F32) - p0[rows, :].astype(F32)))
        resb[t] = total

    with jax.named_scope("s_change0"):
        lax.fori_loop(1, tiles - 1, change0, 0)
        edge_change(0)
        edge_change(tiles - 1)
    with jax.named_scope("s_band1"):
        band_all(p1)
    far(1, halo1)

    def write1(t, slot):
        for j in range(tile // sub):
            out_ref[rows_of(t * tile + j * sub, sub), :] = fresh(t, slot, j).astype(BF)

    with jax.named_scope("s_finish1"):
        finish(1, write1)

    asked.wait_send()
    for copy in halo0 + halo1:
        copy.wait_send()
    for it in range(2):
        span = pl.ds(1, n - 1)
        pltpu.make_async_remote_copy(
            send.at[it, span], recv.at[it, span], ssem.at[it], rsem.at[it, 0],
            device_id=(nxt,), device_id_type=MESH,
        ).wait_send()


def body(labels, seed_mask, band_w, far_block, far_tile, far_count, far_w):
    nodes, classes = labels.shape
    tiles, _, tile, _ = band_w.shape
    _, n, slots, blk, _ = far_w.shape
    hbm = pl.BlockSpec(memory_space=pltpu.HBM)
    vmem = pl.BlockSpec(memory_space=pltpu.VMEM)
    dma = pltpu.SemaphoreType.DMA
    wide = n * slots * blk
    new, old, first = pl.pallas_call(
        functools.partial(kernel, n, tiles, tile, classes, slots, blk),
        out_shape=(
            pltpu.VMEM((nodes, classes), BF),
            pltpu.VMEM((nodes + 2 * tile, classes), BF),
            pltpu.VMEM((tiles, 8, tile), F32),
        ),
        in_specs=[hbm] * 7,
        out_specs=(vmem, vmem, vmem),
        scratch_shapes=[
            pltpu.VMEM((nodes + 2 * tile, classes), BF),
            pltpu.VMEM((nodes // blk, blk, classes), F32),
            pltpu.VMEM((nodes, classes), F32),
            pltpu.VMEM((2, 2, tile, classes), BF),
            pltpu.VMEM((2, n, slots * blk, classes), BF),
            pltpu.VMEM((2, n, slots * blk, classes), BF),
            pltpu.VMEM(band_w.shape, BF),
            pltpu.VMEM((n, slots * blk, tile), BF),
            pltpu.VMEM((n, slots * blk, tile), BF),
            pltpu.VMEM((n // CHUNK, tile, CHUNK * slots * blk), BF),
            pltpu.VMEM((n // CHUNK, tiles, 16, CHUNK * slots * blk), BF),
            pltpu.VMEM((tiles, wide), F32),
            pltpu.VMEM((tile, tile), F32),
            pltpu.VMEM((nodes, tile), F32),
                *[pltpu.VMEM((tile, classes), F32)] * 4,
            *[pltpu.VMEM((tile, tile), F32)] * 4,
            pltpu.VMEM((slots, n), jnp.int32),
            pltpu.VMEM((slots, n), jnp.int32),
            pltpu.VMEM((1, n), jnp.int32),
            pltpu.VMEM((tiles, tile), jnp.int32),
            pltpu.VMEM((n, 1, tile), jnp.int32),
            pltpu.VMEM((n, 1, tile), jnp.int32),
            pltpu.SMEM((n, 1, tile), jnp.int32),
            dma((3,)),
            dma((4,)),
            dma,
            dma,
            dma((n // RUN,)),
            dma((2,)),
            dma((2, n // CHUNK)),
            dma((2, 2)),
            dma((2, 2)),
        ],
        compiler_params=pltpu.CompilerParams(
            collective_id=0, has_side_effects=True, vmem_limit_bytes=51 * 2**20
        ),
    )(
        *(
            pltpu.with_memory_space_constraint(x, pltpu.HBM)
            for x in (
                labels,
                band_w,
                far_w.reshape(n, slots * blk, tile),
                far_block[0].T,
                far_tile[0].T,
                far_count,
                seed_mask.reshape(tiles, tile),
            )
        )
    )
    return pl.pallas_call(
        functools.partial(close, tiles, tile, 32),
        out_shape=(
            jax.ShapeDtypeStruct((nodes, classes), BF),
            jax.ShapeDtypeStruct((2, tiles), F32),
        ),
        in_specs=[vmem] * 3,
        out_specs=(hbm, hbm),
        scratch_shapes=[
            pltpu.VMEM((tiles, 8, tile), F32),
            pltpu.VMEM((2, tiles), F32),
            dma,
            dma,
        ],
        compiler_params=pltpu.CompilerParams(vmem_limit_bytes=4 * 2**20),
    )(*(pltpu.with_memory_space_constraint(x, pltpu.VMEM) for x in (new, old, first)))


def solution(mesh):
    placed = (
        P("node", None),
        P("node"),
        P("node", None, None, None),
        P("node", None, None),
        P("node", None, None),
        P("node", None),
        P("node", None, None, None, None),
    )
    return jax.shard_map(
        body,
        mesh=mesh,
        in_specs=placed,
        out_specs=(P("node", None), P(None, "node")),
        check_vma=False,
    )
```

time: 99.6 us -> 84.5 us (0.85)
  the two profiles are of different devices: /device:TPU:6 before, /device:TPU:1 now
where the time goes in v3:
time: 84.5 us; the launch traced here: 84.4 us
  Pallas kernels  83.8 us (99%)
    pallas_call x1, Pallas kernels, body(): pl.pallas_call(functools.partial(kernel, n, tiles, tile, classes, slots,...  81.4 us
    pallas_call x1, Pallas kernels, body(): pl.pallas_call(functools.partial(close, tiles, tile, 32), out_shape=(jax....  2.31 us

profile of v3, /device:TPU:1, one launch (start us, length us, event | category | flops | bytes accessed | tf_op | source)
XLA Modules:
  0.0 84.4 jit_solution(10126325823398090457)
XLA Ops:
  0.6 81.4 %shard_map.86 = (bf16[4096,512]{1,0:T(8,128)(2,1)S(1)}, bf16[4352,512]{1,0:T(8,128)(2,1)S(1)}, f32[32,8,128]{2,1,0:T(8,128)S(1)}) custom-call(bf16[4096,512]{1,0:T(8,128)(2,1)} %lab_hbm.1, bf16[32,3,128,128]{3,2,1,0:T(8,128)(2,1)} %bw_hbm.1, bf16[128,16,128]{2,1,0:T(8,128)(2,1)} %bitcast.8, s32[2,128]{1,0:T(2,128)} %bitcast.10, s32[2,128]{1,0:T(2,128)} %bitcast.11, ...), custom_call_target="tpu_custom_call" | custom-call | tf_op jit(solution)/shard_map/pallas_call | solution.py:469
  82.1 2.3 %shard_map.87 = (bf16[4096,512]{1,0:T(8,128)(2,1)}, f32[2,32]{1,0:T(2,128)}) custom-call(bf16[4096,512]{1,0:T(8,128)(2,1)S(1)} %get-tuple-element.5.new, bf16[4352,512]{1,0:T(8,128)(2,1)S(1)} %get-tuple-element.6.old, f32[32,8,128]{2,1,0:T(8,128)S(1)} %get-tuple-element.7.first), custom_call_target="tpu_custom_call" | custom-call | tf_op jit(solution)/shard_map/pallas_call | solution.py:529

commit v4 on v3

--- a/solution.py
+++ b/solution.py
@@ -35,9 +35,9 @@
         total = jnp.zeros((8, tile), F32)
         for j in range(tile // sub):
             low = t * tile + j * sub
-            after = new[rows_of(low, sub), :].astype(F32)
-            before = old[pl.ds(pl.multiple_of(tile + low, sub), sub), :].astype(F32)
-            total = total + fold_rows(jnp.abs(after - before))
+            after = new[rows_of(low, sub), :]
+            before = old[pl.ds(pl.multiple_of(tile + low, sub), sub), :]
+            total = total + fold_rows(jnp.abs(after - before).astype(F32))
         second[t] = total
         return carry
 
@@ -55,7 +55,8 @@
     n, tiles, tile, classes, slots, blk,
     lab_hbm, bw_hbm, fw_hbm, fb_hbm, ft_hbm, fc_hbm, sm_hbm,
     out_ref, p1, resb,
-    p0, g32, acc, halo, send, recv, bw, fw, wp, wt, mask, oh, dt, inv, sum0, sum1, sum2, sum3, fac0, fac1, fac2, fac3,
+    p0, g32, acc, halo, send, recv, bw, fw, wp, wt, mask, oh, dt, inv, sum0, sum1, sum2, sum3, sum4, sum5, sum6, sum7,
+    fac0, fac1, fac2, fac3, fac4, fac5, fac6, fac7,
     fb, ft, fc, sm, req, qv, qs,
     load_sem, small_sem, req_ssem, req_rsem, q_sem, ssem, rsem, h_ssem, h_rsem,
 ):
@@ -63,7 +64,16 @@
     nodes = tiles * tile
     pair = slots * blk
     wide = n * pair
-    sums, factors = (sum0, sum1, sum2, sum3), (fac0, fac1, fac2, fac3)
+    def get(ref, row, size):
+        part = pl.ds(pl.multiple_of(row // blk, size // blk), size // blk)
+        return ref[part].reshape(size, ref.shape[2])
+
+    def put(ref, row, size, value):
+        part = pl.ds(pl.multiple_of(row // blk, size // blk), size // blk)
+        ref[part] = value.reshape(size // blk, blk, ref.shape[2])
+
+    sums = (sum0, sum1, sum2, sum3, sum4, sum5, sum6, sum7)
+    factors = (fac0, fac1, fac2, fac3, fac4, fac5, fac6, fac7)
     chunks = n // CHUNK
     kdim = CHUNK * pair
 
@@ -76,12 +86,11 @@
     def target_of(p):
         return plus(me, -p * STEP)
 
-    def far_first(i):
-        return i ^ 84
-
-    def each_peer(step):
-        lax.fori_loop(0, 84, step, 0)
-        lax.fori_loop(85, n, step, 0)
+    def far_first():
+        def hops(s):
+            return sum(min(s // d % 4, 4 - s // d % 4) for d in (2, 8, 32))
+
+        return sorted(range(1, n), key=lambda s: (-hops(s), s))
 
     small = [
         pltpu.make_async_copy(src, dst, small_sem.at[i])
@@ -96,14 +105,9 @@
         copy.start()
     barrier = pltpu.get_barrier_semaphore()
 
-    def greet(i, carry):
-        pl.semaphore_signal(
-            barrier, inc=1, device_id=(plus(me, far_first(i)),), device_id_type=MESH
-        )
-        return carry
-
     with jax.named_scope("s_greet"):
-        each_peer(greet)
+        for distance in far_first():
+            pl.semaphore_signal(barrier, inc=1, device_id=(plus(me, distance),), device_id_type=MESH)
     for copy in small:
         copy.wait()
 
@@ -116,17 +120,12 @@
     with jax.named_scope("s_barrier"):
         pl.semaphore_wait(barrier, n - 1)
 
-    def ask(i, carry):
-        distance = far_first(i)
-        s = plus(me, distance)
-        pltpu.make_async_remote_copy(
-            req.at[s], qv.at[(distance * BACK) & (n - 1)], req_ssem, req_rsem,
-            device_id=(s,), device_id_type=MESH,
-        ).start()
-        return carry
-
     with jax.named_scope("s_ask"):
-        each_peer(ask)
+        for distance in far_first():
+            s = plus(me, distance)
+            pltpu.make_async_remote_copy(
+                req.at[s], qv.at[distance * BACK % n], req_ssem, req_rsem, device_id=(s,), device_id_type=MESH
+            ).start()
     qv[0] = req[me]
     large[1].wait()
 
@@ -214,10 +213,114 @@
     for g in range(runs):
         to_scalar(g).start()
 
+    def band(cur, t):
+        lhs = jnp.concatenate([bw[t, 0], bw[t, 1], bw[t, 2]], axis=1)
+        rhs = cur[pl.ds(pl.multiple_of(t * tile, tile), 3 * tile), :]
+        put(acc, t * tile, tile, jnp.dot(lhs, rhs, preferred_element_type=F32))
+
+    def band_all(cur):
+        def inner(i, carry):
+            band(cur, 2 * i)
+            band(cur, 2 * i + 1)
+            return carry
+
+        lax.fori_loop(0, tiles // 2, inner, 0)
+
+    def edges(it, copies):
+        for copy in copies:
+            copy.wait_recv()
+        for side, t, o in ((0, 0, 0), (1, tiles - 1, 2)):
+            more = jnp.dot(bw[t, o], halo[it, side], preferred_element_type=F32)
+            put(acc, t * tile, tile, get(acc, t * tile, tile) + more)
+
+    def arrived(it, c, low=0):
+        span = pl.ds(c * CHUNK + low, CHUNK - low)
+        pltpu.make_async_remote_copy(
+            send.at[it, span], recv.at[it, span], ssem.at[it], rsem.at[it, c],
+            device_id=(nxt,), device_id_type=MESH,
+        ).wait_recv()
+
+    def product(it, c, t, count):
+        rhs = recv[it, pl.ds(c * CHUNK, CHUNK)].reshape(kdim, classes)
+        weights = wt[c].reshape(tile // 16, 16, kdim)
+        parts = [(weights * mask[c, t + j][None]).reshape(tile, kdim) for j in range(count)]
+        lhs = parts[0] if count == 1 else jnp.concatenate(parts, axis=0)
+        return jnp.dot(lhs, rhs, preferred_element_type=F32)
+
+    group = 16
+
+    def multiply(it, c):
+        def some(g, inner):
+            row, size = g * group * tile, group * tile
+            put(acc, row, size, get(acc, row, size) + product(it, c, g * group, group))
+            return inner
+
+        with jax.named_scope("s_mm"):
+            lax.fori_loop(0, tiles // group, some, 0)
+
+    def far(it, copies):
+        def chunk(c, carry):
+            with jax.named_scope("s_wait"):
+                arrived(it, c)
+            multiply(it, c)
+            return carry
+
+        arrived(it, 0, 1)
+        multiply(it, jnp.int32(0))
+        lax.fori_loop(1, chunks - 1, chunk, 0)
+        edges(it, copies)
+        with jax.named_scope("s_waitlast"):
+            arrived(it, chunks - 1)
+
+    sub = 32
+    reps = classes // tile
+
+    def factor_of(spread, one):
+        square = jnp.sum(spread * spread, axis=1, keepdims=True)
+        mean = square * one * one * (1.0 / classes)
+        return one * lax.rsqrt(jnp.maximum(mean, FLOOR * FLOOR))
+
+    def chosen(spread, factor, signed, given):
+        seeded = jnp.concatenate([signed] * reps, axis=1) < 0.0
+        return jnp.where(seeded, given, spread * jnp.concatenate([factor] * reps, axis=1))
+
+    def scale(it, t, slot):
+        spread = get(acc, t * tile, 2 * tile) + product(it, chunks - 1, t, 2)
+        factor = factor_of(spread, jnp.abs(get(inv, t * tile, 2 * tile)))
+        for k in range(2):
+            part = slice(k * tile, (k + 1) * tile)
+            sums[slot + k][...] = spread[part]
+            factors[slot + k][...] = factor[part]
+
+    def fresh(t, slot, j):
+        part = pl.ds(j * sub, sub)
+        row = t * tile + j * sub
+        given = p0[pl.ds(pl.multiple_of(tile + row, sub), sub), :].astype(F32)
+        return chosen(sums[slot][part, :], factors[slot][part, :], get(inv, row, sub), given)
+
+    fold = fold_rows
+
+    def settle(t):
+        total = jnp.zeros((8, tile), F32)
+        for j in range(tile // sub):
+            row = t * tile + j * sub
+            rows = pl.ds(pl.multiple_of(tile + row, sub), sub)
+            spread, signed = get(acc, row, sub), get(inv, row, sub)
+            given = p0[rows, :].astype(F32)
+            new = chosen(spread, factor_of(spread, jnp.abs(signed)), signed, given).astype(BF)
+            p1[rows, :] = new
+            total = total + fold(jnp.abs(new.astype(F32) - given))
+        resb[t] = total
+
     def exchange(it):
+        def block(b):
+            if it == 0:
+                return g32[b]
+            spread, signed = acc[b], inv[b]
+            return chosen(spread, factor_of(spread, jnp.abs(signed)), signed, g32[b])
+
         def gather(p):
-            blocks = [g32[qs[p, 0, k]] for k in range(slots)]
-            return jnp.concatenate(blocks, axis=0).astype(BF)
+            return jnp.concatenate([block(qs[p, 0, k]) for k in range(slots)], axis=0).astype(BF)
 
         def load(g, low=0):
             if it == 0:
@@ -237,128 +340,52 @@
         def both(g, carry):
             load(g)
             ship(g - 1)
-            if it == 1:
-                low = pl.multiple_of((g // 2 - 1) * 16, 16)
-
-                @pl.when(g % 2 == 0)
-                def _():
-                    for copy in halo_copies(1, p1, low, 16):
-                        copy.start()
-
             return carry
+
+        def both_and_halo(g, carry):
+            low = pl.multiple_of((g - runs // 2) * 16, 16)
+            for copy in halo_copies(1, p1, low, 16):
+                copy.start()
+            return both(g, carry)
 
         zero = jnp.int32(0)
         load(zero, 1)
         recv[it, 0] = gather(0)
         load(zero + 1)
         ship(zero, 1)
-        lax.fori_loop(2, runs, both, 0)
+        if it == 0:
+            lax.fori_loop(2, runs, both, 0)
+        else:
+            lax.fori_loop(2, runs // 2, both, 0)
+            with jax.named_scope("s_edgetiles"):
+                settle(0)
+                settle(tiles - 1)
+            lax.fori_loop(runs // 2, runs, both_and_halo, 0)
         ship(zero + (runs - 1))
-        if it == 1:
-            for copy in halo_copies(1, p1, tile - 16, 16):
-                copy.start()
-
-    def band(cur, t):
-        lhs = jnp.concatenate([bw[t, 0], bw[t, 1], bw[t, 2]], axis=1)
-        rhs = cur[pl.ds(pl.multiple_of(t * tile, tile), 3 * tile), :]
-        acc[rows_of(t * tile, tile), :] = jnp.dot(lhs, rhs, preferred_element_type=F32)
-
-    def band_all(cur):
-        def inner(i, carry):
-            band(cur, 2 * i)
-            band(cur, 2 * i + 1)
-            return carry
-
-        lax.fori_loop(0, tiles // 2, inner, 0)
-
-    def edges(it, copies):
-        for copy in copies:
-            copy.wait_recv()
-        for side, t, o in ((0, 0, 0), (1, tiles - 1, 2)):
-            rows = pl.ds(t * tile, tile)
-            acc[rows, :] = acc[rows, :] + jnp.dot(bw[t, o], halo[it, side], preferred_element_type=F32)
-
-    def arrived(it, c, low=0):
-        span = pl.ds(c * CHUNK + low, CHUNK - low)
-        pltpu.make_async_remote_copy(
-            send.at[it, span], recv.at[it, span], ssem.at[it], rsem.at[it, c],
-            device_id=(nxt,), device_id_type=MESH,
-        ).wait_recv()
-
-    def product(it, c, t, count):
-        rhs = recv[it, pl.ds(c * CHUNK, CHUNK)].reshape(kdim, classes)
-        weights = wt[c].reshape(tile // 16, 16, kdim)
-        parts = [(weights * mask[c, t + j][None]).reshape(tile, kdim) for j in range(count)]
-        lhs = parts[0] if count == 1 else jnp.concatenate(parts, axis=0)
-        return jnp.dot(lhs, rhs, preferred_element_type=F32)
-
-    group = 16
-
-    def far(it, copies):
-        def chunk(c, carry):
-            with jax.named_scope("s_wait"):
-                arrived(it, c)
-            multiply(c)
-            return carry
-
-        def multiply(c):
-            def some(g, inner):
-                rows = rows_of(g * group * tile, group * tile)
-                acc[rows, :] = acc[rows, :] + product(it, c, g * group, group)
-                return inner
-
-            with jax.named_scope("s_mm"):
-                lax.fori_loop(0, tiles // group, some, 0)
-
-        arrived(it, 0, 1)
-        multiply(jnp.int32(0))
-        lax.fori_loop(1, chunks - 1, chunk, 0)
-        edges(it, copies)
-        with jax.named_scope("s_waitlast"):
-            arrived(it, chunks - 1)
-
-    sub = 32
-    reps = classes // tile
-
-    def scale(it, t, slot):
-        spread = acc[rows_of(t * tile, tile), :] + product(it, chunks - 1, t, 1)
-        sums[slot][...] = spread
-        one = jnp.abs(inv[rows_of(t * tile, tile), :])
-        square = jnp.sum(spread * spread, axis=1, keepdims=True)
-        mean = square * one * one * (1.0 / classes)
-        factors[slot][...] = one * lax.rsqrt(jnp.maximum(mean, FLOOR * FLOOR))
-
-    def fresh(t, slot, j):
-        part = pl.ds(j * sub, sub)
-        row = t * tile + j * sub
-        scaled = sums[slot][part, :] * jnp.concatenate([factors[slot][part, :]] * reps, axis=1)
-        seeded = jnp.concatenate([inv[rows_of(row, sub), :]] * reps, axis=1) < 0.0
-        given = p0[pl.ds(pl.multiple_of(tile + row, sub), sub), :].astype(F32)
-        return jnp.where(seeded, given, scaled)
-
-    fold = fold_rows
 
     def finish(it, write):
         def step(i, carry):
-            t = 4 * i
-            scale(it, t + 2, 2)
-            scale(it, t + 3, 3)
-            write(t, 0)
-            write(t + 1, 1)
-            scale(it, t + 4, 0)
-            scale(it, t + 5, 1)
-            write(t + 2, 2)
-            write(t + 3, 3)
+            t = 8 * i
+            for j in (0, 2):
+                scale(it, t + 4 + j, 4 + j)
+                write(t + j, j)
+                write(t + j + 1, j + 1)
+            for j in (0, 2):
+                scale(it, t + 8 + j, j)
+                write(t + 4 + j, 4 + j)
+                write(t + 5 + j, 5 + j)
             return carry
 
-        last = jnp.int32(tiles - 4)
-        scale(it, jnp.int32(0), 0)
-        scale(it, jnp.int32(1), 1)
-        lax.fori_loop(0, tiles // 4 - 1, step, 0)
-        scale(it, last + 2, 2)
-        scale(it, last + 3, 3)
+        for j in (0, 2):
+            scale(it, jnp.int32(j), j)
+        lax.fori_loop(0, tiles // 8 - 1, step, 0)
+        t = jnp.int32(tiles - 8)
+        for j in (0, 2):
+            scale(it, t + 4 + j, 4 + j)
+            write(t + j, j)
+            write(t + j + 1, j + 1)
         for j in range(4):
-            write(last + j, j)
+            write(t + 4 + j, 4 + j)
 
     with jax.named_scope("s_exchange0"):
         exchange(0)
@@ -373,7 +400,7 @@
             seed = jnp.sum(jnp.where(lane == t + tiles, both, 0.0), axis=1, keepdims=True)
             weight = bw[t, 0].astype(F32) + bw[t, 1].astype(F32) + bw[t, 2].astype(F32)
             one = 1.0 / (jnp.sum(weight, axis=1, keepdims=True) + far)
-            inv[rows_of(t * tile, tile), :] = jnp.broadcast_to(jnp.where(seed > 0.5, -one, one), (tile, tile))
+            put(inv, t * tile, tile, jnp.broadcast_to(jnp.where(seed > 0.5, -one, one), (tile, tile)))
         return carry
 
     with jax.named_scope("s_invert"):
@@ -395,47 +422,19 @@
         band_all(p0)
     far(0, halo0)
 
-    def write0(t, slot):
-        for j in range(tile // sub):
-            new = fresh(t, slot, j)
-            g32[pl.ds(t * (tile // blk) + j * (sub // blk), sub // blk)] = new.reshape(sub // blk, blk, classes)
-
-    with jax.named_scope("s_finish0"):
-        finish(0, write0)
-
-    def narrow(t):
-        new = g32[rows_of(t * (tile // blk), tile // blk)].reshape(tile, classes).astype(BF)
-        p1[rows_of(tile + t * tile, tile), :] = new
-
-    narrow(jnp.int32(0))
-    narrow(jnp.int32(tiles - 1))
+    multiply(0, jnp.int32(chunks - 1))
 
     halo1 = halo_copies(1, p1)
     with jax.named_scope("s_exchange1"):
         exchange(1)
 
-    def change0(t, carry):
-        total = jnp.zeros((8, tile), F32)
-        for j in range(tile // sub):
-            rows = pl.ds(pl.multiple_of(tile + t * tile + j * sub, sub), sub)
-            part = pl.ds(t * (tile // blk) + j * (sub // blk), sub // blk)
-            new = g32[part].reshape(sub, classes).astype(BF)
-            p1[rows, :] = new
-            total = total + fold(jnp.abs(new.astype(F32) - p0[rows, :].astype(F32)))
-        resb[t] = total
-        return carry
-
-    def edge_change(t):
-        total = jnp.zeros((8, tile), F32)
-        for j in range(tile // sub):
-            rows = pl.ds(tile + t * tile + j * sub, sub)
-            total = total + fold(jnp.abs(p1[rows, :].astype(F32) - p0[rows, :].astype(F32)))
-        resb[t] = total
-
-    with jax.named_scope("s_change0"):
-        lax.fori_loop(1, tiles - 1, change0, 0)
-        edge_change(0)
-        edge_change(tiles - 1)
+    def settle_two(i, carry):
+        settle(2 * i + 1)
+        settle(2 * i + 2)
+        return carry
+
+    with jax.named_scope("s_settle"):
+        lax.fori_loop(0, tiles // 2 - 1, settle_two, 0)
     with jax.named_scope("s_band1"):
         band_all(p1)
     far(1, halo1)
@@ -478,7 +477,7 @@
         scratch_shapes=[
             pltpu.VMEM((nodes + 2 * tile, classes), BF),
             pltpu.VMEM((nodes // blk, blk, classes), F32),
-            pltpu.VMEM((nodes, classes), F32),
+            pltpu.VMEM((nodes // blk, blk, classes), F32),
             pltpu.VMEM((2, 2, tile, classes), BF),
             pltpu.VMEM((2, n, slots * blk, classes), BF),
             pltpu.VMEM((2, n, slots * blk, classes), BF),
@@ -489,9 +488,9 @@
             pltpu.VMEM((n // CHUNK, tiles, 16, CHUNK * slots * blk), BF),
             pltpu.VMEM((tiles, wide), F32),
             pltpu.VMEM((tile, tile), F32),
-            pltpu.VMEM((nodes, tile), F32),
-                *[pltpu.VMEM((tile, classes), F32)] * 4,
-            *[pltpu.VMEM((tile, tile), F32)] * 4,
+            pltpu.VMEM((nodes // blk, blk, tile), F32),
+                *[pltpu.VMEM((tile, classes), F32)] * 8,
+            *[pltpu.VMEM((tile, tile), F32)] * 8,
             pltpu.VMEM((slots, n), jnp.int32),
             pltpu.VMEM((slots, n), jnp.int32),
             pltpu.VMEM((1, n), jnp.int32),
@@ -510,7 +509,7 @@
             dma((2, 2)),
         ],
         compiler_params=pltpu.CompilerParams(
-            collective_id=0, has_side_effects=True, vmem_limit_bytes=51 * 2**20
+            collective_id=0, has_side_effects=True, vmem_limit_bytes=52 * 2**20
         ),
     )(
         *(

time: 84.5 us -> 82.2 us (0.973)
  Pallas kernels: 83.8 us -> 81.5 us
    pallas_call x1, Pallas kernels: 81.4 us -> 79.4 us  [body(): pl.pallas_call(functools.partial(kernel, n, tiles, tile, classes, slots,...]
where the time goes in v4:
time: 82.2 us; the launch traced here: 82.1 us
  Pallas kernels  81.5 us (99%)
    pallas_call x1, Pallas kernels, body(): pl.pallas_call(functools.partial(kernel, n, tiles, tile, classes, slots,...  79.4 us
    pallas_call x1, Pallas kernels, body(): pl.pallas_call(functools.partial(close, tiles, tile, 32), out_shape=(jax....  2.03 us

profile of v4, /device:TPU:1, one launch (start us, length us, event | category | flops | bytes accessed | tf_op | source)
XLA Modules:
  0.0 82.1 jit_solution(7029214020135079053)
XLA Ops:
  0.6 79.4 %shard_map.86 = (bf16[4096,512]{1,0:T(8,128)(2,1)S(1)}, bf16[4352,512]{1,0:T(8,128)(2,1)S(1)}, f32[32,8,128]{2,1,0:T(8,128)S(1)}) custom-call(bf16[4096,512]{1,0:T(8,128)(2,1)} %lab_hbm.1, bf16[32,3,128,128]{3,2,1,0:T(8,128)(2,1)} %bw_hbm.1, bf16[128,16,128]{2,1,0:T(8,128)(2,1)} %bitcast.8, s32[2,128]{1,0:T(2,128)} %bitcast.10, s32[2,128]{1,0:T(2,128)} %bitcast.11, ...), custom_call_target="tpu_custom_call" | custom-call | tf_op jit(solution)/shard_map/pallas_call | solution.py:468
  80.1 2.0 %shard_map.87 = (bf16[4096,512]{1,0:T(8,128)(2,1)}, f32[2,32]{1,0:T(2,128)}) custom-call(bf16[4096,512]{1,0:T(8,128)(2,1)S(1)} %get-tuple-element.5.new, bf16[4352,512]{1,0:T(8,128)(2,1)S(1)} %get-tuple-element.6.old, f32[32,8,128]{2,1,0:T(8,128)S(1)} %get-tuple-element.7.first), custom_call_target="tpu_custom_call" | custom-call | tf_op jit(solution)/shard_map/pallas_call | solution.py:528

commit v5 on v4

--- a/solution.py
+++ b/solution.py
@@ -55,10 +55,10 @@
     n, tiles, tile, classes, slots, blk,
     lab_hbm, bw_hbm, fw_hbm, fb_hbm, ft_hbm, fc_hbm, sm_hbm,
     out_ref, p1, resb,
-    p0, g32, acc, halo, send, recv, bw, fw, wp, wt, mask, oh, dt, inv, sum0, sum1, sum2, sum3, sum4, sum5, sum6, sum7,
+    p0, g32, acc, halo, send, recv, fsend, frecv, wf, bw, fw, wp, wt, mask, oh, dt, inv, sum0, sum1, sum2, sum3, sum4, sum5, sum6, sum7,
     fac0, fac1, fac2, fac3, fac4, fac5, fac6, fac7,
     fb, ft, fc, sm, req, qv, qs,
-    load_sem, small_sem, req_ssem, req_rsem, q_sem, ssem, rsem, h_ssem, h_rsem,
+    load_sem, small_sem, req_ssem, req_rsem, q_sem, ssem, rsem, f_ssem, f_rsem, h_ssem, h_rsem,
 ):
     me = lax.axis_index("node")
     nodes = tiles * tile
@@ -75,6 +75,7 @@
     sums = (sum0, sum1, sum2, sum3, sum4, sum5, sum6, sum7)
     factors = (fac0, fac1, fac2, fac3, fac4, fac5, fac6, fac7)
     chunks = n // CHUNK
+    half = classes // 2
     kdim = CHUNK * pair
 
     def plus(a, b):
@@ -233,59 +234,72 @@
             more = jnp.dot(bw[t, o], halo[it, side], preferred_element_type=F32)
             put(acc, t * tile, tile, get(acc, t * tile, tile) + more)
 
-    def arrived(it, c, low=0):
+    def arrived(it, h, c, low=0):
         span = pl.ds(c * CHUNK + low, CHUNK - low)
         pltpu.make_async_remote_copy(
-            send.at[it, span], recv.at[it, span], ssem.at[it], rsem.at[it, c],
+            send.at[it, h, span], recv.at[it, h, span], ssem.at[it, h], rsem.at[it, h, c],
             device_id=(nxt,), device_id_type=MESH,
         ).wait_recv()
 
-    def product(it, c, t, count):
-        rhs = recv[it, pl.ds(c * CHUNK, CHUNK)].reshape(kdim, classes)
-        weights = wt[c].reshape(tile // 16, 16, kdim)
+    def product(it, h, c, t, count):
+        span = pl.ds(c * CHUNK, CHUNK)
+        if h is None:
+            rhs = jnp.concatenate([recv[it, k, span].reshape(kdim, half) for k in range(2)], axis=1)
+        else:
+            rhs = recv[it, h, span].reshape(kdim, half)
+        weights = (wt if it == 0 else wf)[c].reshape(tile // 16, 16, kdim)
         parts = [(weights * mask[c, t + j][None]).reshape(tile, kdim) for j in range(count)]
         lhs = parts[0] if count == 1 else jnp.concatenate(parts, axis=0)
         return jnp.dot(lhs, rhs, preferred_element_type=F32)
 
     group = 16
 
-    def multiply(it, c):
+    def multiply(it, h, c):
+        cols = pl.ds(0, classes) if h is None else pl.ds(h * half, half)
+
         def some(g, inner):
-            row, size = g * group * tile, group * tile
-            put(acc, row, size, get(acc, row, size) + product(it, c, g * group, group))
+            size = group * tile // blk
+            part = pl.ds(pl.multiple_of(g * size, size), size)
+            more = product(it, h, c, g * group, group)
+            acc[part, :, cols] = acc[part, :, cols] + more.reshape(size, blk, more.shape[1])
             return inner
 
         with jax.named_scope("s_mm"):
             lax.fori_loop(0, tiles // group, some, 0)
 
-    def far(it, copies):
+    def far(it, h, count):
+        halves = (0, 1) if h is None else (h,)
+
         def chunk(c, carry):
             with jax.named_scope("s_wait"):
-                arrived(it, c)
-            multiply(it, c)
-            return carry
-
-        arrived(it, 0, 1)
-        multiply(it, jnp.int32(0))
-        lax.fori_loop(1, chunks - 1, chunk, 0)
-        edges(it, copies)
-        with jax.named_scope("s_waitlast"):
-            arrived(it, chunks - 1)
+                for k in halves:
+                    arrived(it, k, c)
+            multiply(it, h, c)
+            return carry
+
+        for k in halves:
+            arrived(it, k, 0, 1)
+        multiply(it, h, jnp.int32(0))
+        lax.fori_loop(1, count, chunk, 0)
 
     sub = 32
     reps = classes // tile
 
-    def factor_of(spread, one):
+    def lift(spread, one):
         square = jnp.sum(spread * spread, axis=1, keepdims=True)
         mean = square * one * one * (1.0 / classes)
-        return one * lax.rsqrt(jnp.maximum(mean, FLOOR * FLOOR))
+        return lax.rsqrt(jnp.maximum(mean, FLOOR * FLOOR))
+
+    def factor_of(spread, one):
+        return one * lift(spread, one)
 
     def chosen(spread, factor, signed, given):
+        reps = spread.shape[1] // tile
         seeded = jnp.concatenate([signed] * reps, axis=1) < 0.0
         return jnp.where(seeded, given, spread * jnp.concatenate([factor] * reps, axis=1))
 
     def scale(it, t, slot):
-        spread = get(acc, t * tile, 2 * tile) + product(it, chunks - 1, t, 2)
+        spread = get(acc, t * tile, 2 * tile) + product(it, None, chunks - 1, t, 2)
         factor = factor_of(spread, jnp.abs(get(inv, t * tile, 2 * tile)))
         for k in range(2):
             part = slice(k * tile, (k + 1) * tile)
@@ -312,34 +326,62 @@
             total = total + fold(jnp.abs(new.astype(F32) - given))
         resb[t] = total
 
-    def exchange(it):
-        def block(b):
-            if it == 0:
-                return g32[b]
-            spread, signed = acc[b], inv[b]
-            return chosen(spread, factor_of(spread, jnp.abs(signed)), signed, g32[b])
-
-        def gather(p):
-            return jnp.concatenate([block(qs[p, 0, k]) for k in range(slots)], axis=0).astype(BF)
-
+    def ship(it, h, g, low=0):
+        for j in range(low, RUN):
+            p = g * RUN + j
+            pltpu.make_async_remote_copy(
+                send.at[it, h, p], recv.at[it, h, p], ssem.at[it, h], rsem.at[it, h, g // (CHUNK // RUN)],
+                device_id=(target_of(p),), device_id_type=MESH,
+            ).start()
+
+    def pair_of(block, p):
+        return jnp.concatenate([block(qs[p, 0, k]) for k in range(slots)], axis=0).astype(BF)
+
+    zero = jnp.int32(0)
+
+    def exchange_labels():
         def load(g, low=0):
-            if it == 0:
-                to_scalar(g).wait()
+            to_scalar(g).wait()
             for j in range(low, RUN):
-                send[it, g * RUN + j] = gather(g * RUN + j)
-
-        def ship(g, low=0):
-            c = g // (CHUNK // RUN)
-            for j in range(low, RUN):
-                p = g * RUN + j
-                pltpu.make_async_remote_copy(
-                    send.at[it, p], recv.at[it, p], ssem.at[it], rsem.at[it, c],
-                    device_id=(target_of(p),), device_id_type=MESH,
-                ).start()
+                rows = pair_of(lambda b: g32[b], g * RUN + j)
+                send[0, 0, g * RUN + j] = rows[:, :half]
+                send[0, 1, g * RUN + j] = rows[:, half:]
 
         def both(g, carry):
             load(g)
-            ship(g - 1)
+            ship(0, 0, g - 1)
+            return carry
+
+        def rest(g, carry):
+            ship(0, 1, g)
+            return carry
+
+        load(zero, 1)
+        own = pair_of(lambda b: g32[b], 0)
+        recv[0, 0, 0] = own[:, :half]
+        recv[0, 1, 0] = own[:, half:]
+        load(zero + 1)
+        ship(0, 0, zero, 1)
+        lax.fori_loop(2, runs, both, 0)
+        ship(0, 0, zero + (runs - 1))
+        ship(0, 1, zero, 1)
+        lax.fori_loop(1, runs, rest, 0)
+
+    def gather_averages(h, g, low=0):
+        def block(b):
+            signed = inv[b]
+            cols = slice(h * half, (h + 1) * half)
+            return chosen(acc[b][:, cols], jnp.abs(signed), signed, g32[b][:, cols])
+
+        for j in range(low, RUN):
+            send[1, h, g * RUN + j] = pair_of(block, g * RUN + j)
+        if isinstance(g, int) and g == 0:
+            recv[1, h, 0] = pair_of(block, 0)
+
+    def exchange_averages(h):
+        def both(g, carry):
+            gather_averages(h, g)
+            ship(1, h, g - 1)
             return carry
 
         def both_and_halo(g, carry):
@@ -348,20 +390,64 @@
                 copy.start()
             return both(g, carry)
 
-        zero = jnp.int32(0)
-        load(zero, 1)
-        recv[it, 0] = gather(0)
-        load(zero + 1)
-        ship(zero, 1)
-        if it == 0:
-            lax.fori_loop(2, runs, both, 0)
-        else:
-            lax.fori_loop(2, runs // 2, both, 0)
-            with jax.named_scope("s_edgetiles"):
-                settle(0)
-                settle(tiles - 1)
-            lax.fori_loop(runs // 2, runs, both_and_halo, 0)
-        ship(zero + (runs - 1))
+        gather_averages(h, 0, 1)
+        gather_averages(h, zero + 1)
+        ship(1, h, zero, 1)
+        lax.fori_loop(2, runs // 2, both, 0)
+        if h == 1:
+            settle(0)
+            settle(tiles - 1)
+        lax.fori_loop(runs // 2, runs, both_and_halo if h == 1 else both, 0)
+        ship(1, h, zero + (runs - 1))
+
+    def exchange_lifts():
+        def load(g, carry):
+            lifts = []
+            for j in range(RUN):
+                for k in range(slots):
+                    b = qs[g * RUN + j, 0, k]
+                    signed = inv[b]
+                    lifts.append(jnp.where(signed < 0.0, 1.0, lift(acc[b], jnp.abs(signed))))
+            fsend[g] = jnp.concatenate(lifts, axis=0).T[:1]
+            return carry
+
+        def tell(g, low=0):
+            for j in range(low, RUN):
+                p = g * RUN + j
+                pltpu.make_async_remote_copy(
+                    fsend.at[g], frecv.at[p], f_ssem, f_rsem, device_id=(target_of(p),), device_id_type=MESH
+                ).start()
+
+        def load_and_tell(g, carry):
+            load(g, carry)
+            tell(g - 1)
+            return carry
+
+        load(zero, 0)
+        frecv[0] = fsend[0]
+        load(zero + 1, 0)
+        tell(zero, 1)
+        lax.fori_loop(2, runs, load_and_tell, 0)
+        tell(zero + (runs - 1))
+
+    def told():
+        pltpu.make_async_remote_copy(
+            frecv.at[pl.ds(1, n - 1)], frecv.at[pl.ds(1, n - 1)], f_ssem, f_rsem,
+            device_id=(nxt,), device_id_type=MESH,
+        ).wait_recv()
+        place_of = lax.broadcasted_iota(jnp.int32, (1, tile), 1) // pair
+
+        def apply(c, carry):
+            lanes = []
+            for i in range(CHUNK // RUN):
+                row = jnp.zeros((1, tile), F32)
+                for j in range(RUN):
+                    row = jnp.where(place_of == j, frecv[c * CHUNK + i * RUN + j], row)
+                lanes.append(row)
+            wf[c] = (wt[c].astype(F32) * jnp.concatenate(lanes, axis=1)).astype(BF)
+            return carry
+
+        lax.fori_loop(0, chunks, apply, 0)
 
     def finish(it, write):
         def step(i, carry):
@@ -388,7 +474,7 @@
             write(t + 4 + j, 4 + j)
 
     with jax.named_scope("s_exchange0"):
-        exchange(0)
+        exchange_labels()
 
     large[2].wait()
 
@@ -420,24 +506,34 @@
         lax.fori_loop(0, chunks, spread_mask, 0)
     with jax.named_scope("s_band0"):
         band_all(p0)
-    far(0, halo0)
-
-    multiply(0, jnp.int32(chunks - 1))
+    far(0, 0, chunks)
+    edges(0, halo0)
+    with jax.named_scope("s_averages"):
+        exchange_averages(0)
+    far(0, 1, chunks)
 
     halo1 = halo_copies(1, p1)
     with jax.named_scope("s_exchange1"):
-        exchange(1)
-
-    def settle_two(i, carry):
-        settle(2 * i + 1)
-        settle(2 * i + 2)
+        exchange_lifts()
+        with jax.named_scope("s_second"):
+            exchange_averages(1)
+
+    def settle_five(i, carry):
+        for j in range(5):
+            settle(5 * i + 1 + j)
         return carry
 
     with jax.named_scope("s_settle"):
-        lax.fori_loop(0, tiles // 2 - 1, settle_two, 0)
+        lax.fori_loop(0, (tiles - 2) // 5, settle_five, 0)
     with jax.named_scope("s_band1"):
         band_all(p1)
-    far(1, halo1)
+    with jax.named_scope("s_told"):
+        told()
+    far(1, None, chunks - 1)
+    edges(1, halo1)
+    with jax.named_scope("s_waitlast"):
+        for h in range(2):
+            arrived(1, h, chunks - 1)
 
     def write1(t, slot):
         for j in range(tile // sub):
@@ -449,12 +545,16 @@
     asked.wait_send()
     for copy in halo0 + halo1:
         copy.wait_send()
+    span = pl.ds(1, n - 1)
     for it in range(2):
-        span = pl.ds(1, n - 1)
-        pltpu.make_async_remote_copy(
-            send.at[it, span], recv.at[it, span], ssem.at[it], rsem.at[it, 0],
-            device_id=(nxt,), device_id_type=MESH,
-        ).wait_send()
+        for h in range(2):
+            pltpu.make_async_remote_copy(
+                send.at[it, h, span], recv.at[it, h, span], ssem.at[it, h], rsem.at[it, h, 0],
+                device_id=(nxt,), device_id_type=MESH,
+            ).wait_send()
+    pltpu.make_async_remote_copy(
+        frecv.at[span], frecv.at[span], f_ssem, f_rsem, device_id=(nxt,), device_id_type=MESH
+    ).wait_send()
 
 
 def body(labels, seed_mask, band_w, far_block, far_tile, far_count, far_w):
@@ -479,8 +579,11 @@
             pltpu.VMEM((nodes // blk, blk, classes), F32),
             pltpu.VMEM((nodes // blk, blk, classes), F32),
             pltpu.VMEM((2, 2, tile, classes), BF),
-            pltpu.VMEM((2, n, slots * blk, classes), BF),
-            pltpu.VMEM((2, n, slots * blk, classes), BF),
+            pltpu.VMEM((2, 2, n, slots * blk, classes // 2), BF),
+            pltpu.VMEM((2, 2, n, slots * blk, classes // 2), BF),
+            pltpu.VMEM((n // RUN, 1, tile), F32),
+            pltpu.VMEM((n, 1, tile), F32),
+            pltpu.VMEM((n // CHUNK, tile, CHUNK * slots * blk), BF),
             pltpu.VMEM(band_w.shape, BF),
             pltpu.VMEM((n, slots * blk, tile), BF),
             pltpu.VMEM((n, slots * blk, tile), BF),
@@ -503,8 +606,10 @@
             dma,
             dma,
             dma((n // RUN,)),
-            dma((2,)),
-            dma((2, n // CHUNK)),
+            dma((2, 2)),
+            dma((2, 2, n // CHUNK)),
+            dma,
+            dma,
             dma((2, 2)),
             dma((2, 2)),
         ],

time: 82.2 us -> 77.7 us (0.945)
  the two profiles are of different devices: /device:TPU:1 before, /device:TPU:7 now
where the time goes in v5:
time: 77.7 us; the launch traced here: 77.6 us
  Pallas kernels  76.9 us (99%)
    pallas_call x1, Pallas kernels, body(): pl.pallas_call(functools.partial(kernel, n, tiles, tile, classes, slots,...  74.9 us
    pallas_call x1, Pallas kernels, body(): pl.pallas_call(functools.partial(close, tiles, tile, 32), out_shape=(jax....  2.03 us

profile of v5, /device:TPU:7, one launch (start us, length us, event | category | flops | bytes accessed | tf_op | source)
XLA Modules:
  0.0 77.6 jit_solution(17233009520377720181)
XLA Ops:
  0.6 74.9 %shard_map.86 = (bf16[4096,512]{1,0:T(8,128)(2,1)S(1)}, bf16[4352,512]{1,0:T(8,128)(2,1)S(1)}, f32[32,8,128]{2,1,0:T(8,128)S(1)}) custom-call(bf16[4096,512]{1,0:T(8,128)(2,1)} %lab_hbm.1, bf16[32,3,128,128]{3,2,1,0:T(8,128)(2,1)} %bw_hbm.1, bf16[128,16,128]{2,1,0:T(8,128)(2,1)} %bitcast.8, s32[2,128]{1,0:T(2,128)} %bitcast.10, s32[2,128]{1,0:T(2,128)} %bitcast.11, ...), custom_call_target="tpu_custom_call" | custom-call | tf_op jit(solution)/shard_map/pallas_call | solution.py:568
  75.5 2.0 %shard_map.87 = (bf16[4096,512]{1,0:T(8,128)(2,1)}, f32[2,32]{1,0:T(2,128)}) custom-call(bf16[4096,512]{1,0:T(8,128)(2,1)S(1)} %get-tuple-element.5.new, bf16[4352,512]{1,0:T(8,128)(2,1)S(1)} %get-tuple-element.6.old, f32[32,8,128]{2,1,0:T(8,128)S(1)} %get-tuple-element.7.first), custom_call_target="tpu_custom_call" | custom-call | tf_op jit(solution)/shard_map/pallas_call | solution.py:633

commit v6 on v5

--- a/solution.py
+++ b/solution.py
@@ -55,7 +55,7 @@
     n, tiles, tile, classes, slots, blk,
     lab_hbm, bw_hbm, fw_hbm, fb_hbm, ft_hbm, fc_hbm, sm_hbm,
     out_ref, p1, resb,
-    p0, g32, acc, halo, send, recv, fsend, frecv, wf, bw, fw, wp, wt, mask, oh, dt, inv, sum0, sum1, sum2, sum3, sum4, sum5, sum6, sum7,
+    p0, g32, acc, halo, send, recv, fsend, frecv, wf, bw, fw, wp, wt, mask, oh, dt, inv, ups, sum0, sum1, sum2, sum3, sum4, sum5, sum6, sum7,
     fac0, fac1, fac2, fac3, fac4, fac5, fac6, fac7,
     fb, ft, fc, sm, req, qv, qs,
     load_sem, small_sem, req_ssem, req_rsem, q_sem, ssem, rsem, f_ssem, f_rsem, h_ssem, h_rsem,
@@ -221,11 +221,11 @@
 
     def band_all(cur):
         def inner(i, carry):
-            band(cur, 2 * i)
-            band(cur, 2 * i + 1)
-            return carry
-
-        lax.fori_loop(0, tiles // 2, inner, 0)
+            for j in range(8):
+                band(cur, 8 * i + j)
+            return carry
+
+        lax.fori_loop(0, tiles // 8, inner, 0)
 
     def edges(it, copies):
         for copy in copies:
@@ -252,7 +252,7 @@
         lhs = parts[0] if count == 1 else jnp.concatenate(parts, axis=0)
         return jnp.dot(lhs, rhs, preferred_element_type=F32)
 
-    group = 16
+    group = tiles
 
     def multiply(it, h, c):
         cols = pl.ds(0, classes) if h is None else pl.ds(h * half, half)
@@ -321,7 +321,7 @@
             rows = pl.ds(pl.multiple_of(tile + row, sub), sub)
             spread, signed = get(acc, row, sub), get(inv, row, sub)
             given = p0[rows, :].astype(F32)
-            new = chosen(spread, factor_of(spread, jnp.abs(signed)), signed, given).astype(BF)
+            new = chosen(spread, jnp.abs(signed) * get(ups, row, sub), signed, given).astype(BF)
             p1[rows, :] = new
             total = total + fold(jnp.abs(new.astype(F32) - given))
         resb[t] = total
@@ -405,9 +405,7 @@
             lifts = []
             for j in range(RUN):
                 for k in range(slots):
-                    b = qs[g * RUN + j, 0, k]
-                    signed = inv[b]
-                    lifts.append(jnp.where(signed < 0.0, 1.0, lift(acc[b], jnp.abs(signed))))
+                    lifts.append(ups[qs[g * RUN + j, 0, k]])
             fsend[g] = jnp.concatenate(lifts, axis=0).T[:1]
             return carry
 
@@ -423,6 +421,15 @@
             tell(g - 1)
             return carry
 
+        def measure(i, carry):
+            for j in range(8):
+                row = (8 * i + j) * tile
+                signed = get(inv, row, tile)
+                put(ups, row, tile, jnp.where(signed < 0.0, 1.0, lift(get(acc, row, tile), jnp.abs(signed))))
+            return carry
+
+        with jax.named_scope("s_measure"):
+            lax.fori_loop(0, tiles // 8, measure, 0)
         load(zero, 0)
         frecv[0] = fsend[0]
         load(zero + 1, 0)
@@ -529,7 +536,8 @@
         band_all(p1)
     with jax.named_scope("s_told"):
         told()
-    far(1, None, chunks - 1)
+    far(1, 0, chunks - 1)
+    far(1, 1, chunks - 1)
     edges(1, halo1)
     with jax.named_scope("s_waitlast"):
         for h in range(2):
@@ -592,6 +600,7 @@
             pltpu.VMEM((tiles, wide), F32),
             pltpu.VMEM((tile, tile), F32),
             pltpu.VMEM((nodes // blk, blk, tile), F32),
+            pltpu.VMEM((nodes // blk, blk, tile), F32),
                 *[pltpu.VMEM((tile, classes), F32)] * 8,
             *[pltpu.VMEM((tile, tile), F32)] * 8,
             pltpu.VMEM((slots, n), jnp.int32),
@@ -614,7 +623,7 @@
             dma((2, 2)),
         ],
         compiler_params=pltpu.CompilerParams(
-            collective_id=0, has_side_effects=True, vmem_limit_bytes=52 * 2**20
+            collective_id=0, has_side_effects=True, vmem_limit_bytes=54 * 2**20
         ),
     )(
         *(

time: 77.7 us -> 74.8 us (0.963)
  the two profiles are of different devices: /device:TPU:7 before, /device:TPU:1 now
where the time goes in v6:
time: 74.8 us; the launch traced here: 74.7 us
  Pallas kernels  74.1 us (99%)
    pallas_call x1, Pallas kernels, body(): pl.pallas_call(functools.partial(kernel, n, tiles, tile, classes, slots,...  72 us
    pallas_call x1, Pallas kernels, body(): pl.pallas_call(functools.partial(close, tiles, tile, 32), out_shape=(jax....  2.03 us

profile of v6, /device:TPU:1, one launch (start us, length us, event | category | flops | bytes accessed | tf_op | source)
XLA Modules:
  0.0 74.7 jit_solution(11568021107789772687)
XLA Ops:
  0.6 72.0 %shard_map.86 = (bf16[4096,512]{1,0:T(8,128)(2,1)S(1)}, bf16[4352,512]{1,0:T(8,128)(2,1)S(1)}, f32[32,8,128]{2,1,0:T(8,128)S(1)}) custom-call(bf16[4096,512]{1,0:T(8,128)(2,1)} %lab_hbm.1, bf16[32,3,128,128]{3,2,1,0:T(8,128)(2,1)} %bw_hbm.1, bf16[128,16,128]{2,1,0:T(8,128)(2,1)} %bitcast.8, s32[2,128]{1,0:T(2,128)} %bitcast.10, s32[2,128]{1,0:T(2,128)} %bitcast.11, ...), custom_call_target="tpu_custom_call" | custom-call | tf_op jit(solution)/shard_map/pallas_call | solution.py:576
  72.7 2.0 %shard_map.87 = (bf16[4096,512]{1,0:T(8,128)(2,1)}, f32[2,32]{1,0:T(2,128)}) custom-call(bf16[4096,512]{1,0:T(8,128)(2,1)S(1)} %get-tuple-element.5.new, bf16[4352,512]{1,0:T(8,128)(2,1)S(1)} %get-tuple-element.6.old, f32[32,8,128]{2,1,0:T(8,128)S(1)} %get-tuple-element.7.first), custom_call_target="tpu_custom_call" | custom-call | tf_op jit(solution)/shard_map/pallas_call | solution.py:642
